TPU v7x, 32 devices: a whole 2x2x4 slice. The times are simulated.
32 devices in a mesh: dp: 8 (over z, x), mp: 4 (over y, core).
Axes of the slice: x: 2, y: 2, z: 4, core: 2. Of those that a mesh axis runs over, the one named last changes fastest.
Arguments:
- activations: bfloat16 [1024, 1024], P('dp'), may hold values from -6 to 6
- cotangents: bfloat16 [1024, 4096], P('dp', 'mp'), may hold values from -1200 to 1200
- owners: int32 [4], replicated, may hold values from 0 to 7, as said below
Outputs:
- update: bfloat16 [1024, 4096], P('dp', 'mp')
- roots: float32 [4096, 2048], P('dp', 'mp')
- graft: float32 [], replicated
Inputs may be any that keep to these rules, and one draw needn't show every extreme that they name: The left root of block b is computed at dp index owners[b] and its right root at owners[b] with its lowest bit flipped; every dp index computes exactly one root.
All inputs are finite; a program needn't handle non-finite values.
Results may differ from a plain program's by a relative error of at most 0.00045.
Values may be sent and summed in bfloat16 or wider, within the bound.
A program may use at most 64 MiB of HBM per device.

v0:
```python
import math

import jax
import jax.numpy as jnp
from jax import lax
from jax.sharding import PartitionSpec as P

B = 512
CB = 2
ITERS = 3


def partner_2(value, axis, bit):
    return lax.ppermute(value, axis, [(i, i ^ 1 << bit) for i in range(lax.axis_size(axis))])


def product(left, right):
    return jnp.dot(left, right, precision=lax.Precision.HIGHEST, preferred_element_type=jnp.float32)


def statistic_of(operand):
    gram = product(operand, operand.T)
    ridge = 0.1 * (jnp.sum(operand * operand) / operand.shape[0] + 1.0)
    return gram + ridge * jnp.eye(operand.shape[0], dtype=jnp.float32)


def inverse_root(statistic):
    eye_matrix = jnp.eye(statistic.shape[0], dtype=jnp.float32)
    magnitude = jnp.sqrt(jnp.sum(statistic * statistic))
    current = statistic / magnitude
    result = eye_matrix
    for step in range(ITERS):
        factor = (5.0 * eye_matrix - current) * 0.25
        if step == 0:
            result = factor * magnitude ** (-0.25)
        else:
            result = product(result, factor)
        if step + 1 < ITERS:
            square = product(factor, factor)
            current = product(product(square, square), current)
    return result


def half_squares(matrix, upper_half):
    row_ids = jnp.arange(matrix.shape[0], dtype=jnp.int32)
    in_half = (row_ids < matrix.shape[0] // 2) == upper_half
    return jnp.sum(jnp.where(in_half[:, None], matrix * matrix, 0.0), axis=0)


def on_device(activations, cotangents, owners):
    my_index = lax.axis_index("dp")
    dp_count = lax.axis_size("dp")
    local_tokens = activations.shape[0]
    row_blocks = activations.shape[1] // B
    block_count = owners.shape[0]
    dest_index = jnp.arange(dp_count, dtype=jnp.int32)
    partner = owners + 1 - 2 * (owners % 2)
    left_match = owners[None, :] == dest_index[:, None]
    right_match = partner[None, :] == dest_index[:, None]
    block_ids = jnp.arange(block_count, dtype=jnp.int32)
    owned = jnp.sum(jnp.where(left_match | right_match, block_ids[None, :], 0), axis=1)
    left_dest = jnp.any(left_match, axis=1)
    row_dest = owned // CB
    col_dest = owned % CB
    my_block = owned[my_index]
    my_left = left_dest[my_index]
    token_rows = jnp.take(activations.reshape(local_tokens, row_blocks, B), row_dest, axis=1)
    cotangent_rows = jnp.take(cotangents.reshape(local_tokens, CB, B), col_dest, axis=1)
    mixed = jnp.where(left_dest[None, :, None], token_rows, cotangent_rows)
    received = lax.all_to_all(mixed, "dp", split_axis=1, concat_axis=0, tiled=True)[:, 0, :]
    partner_part = partner_2(received, "dp", 0)
    inputs_block = jnp.where(my_left, received, partner_part)
    outputs_block = jnp.where(my_left, partner_part, received)
    all_tokens = inputs_block.shape[0]
    gradient = lax.dot_general(
        inputs_block, outputs_block, (((0,), (0,)), ((), ())), preferred_element_type=jnp.float32
    ) / math.sqrt(all_tokens)
    grad_share = half_squares(gradient, my_left)
    grad_total = jnp.sum(lax.psum(grad_share, ("dp", "mp")))
    oriented = jnp.where(my_left, gradient, gradient.T)
    root = inverse_root(statistic_of(oriented))
    other_root = partner_2(root, "dp", 0)
    left_root = jnp.where(my_left, root, other_root)
    right_root = jnp.where(my_left, other_root, root)
    preconditioned = product(left_root, product(gradient, right_root))
    precond_share = half_squares(preconditioned, my_left)
    precond_total = jnp.sum(lax.psum(precond_share, ("dp", "mp")))
    graft = jnp.sqrt(grad_total / jnp.maximum(precond_total, 1.0))
    scaled = jnp.where(my_left, graft * preconditioned, 0.0).astype(jnp.bfloat16)
    dest_rows = activations.shape[1] // dp_count
    pieces = scaled.reshape(B // dest_rows, dest_rows, B)
    outgoing = jnp.zeros((dp_count, dest_rows, B), jnp.bfloat16)
    first_dest = my_block // CB * (B // dest_rows)
    outgoing = lax.dynamic_update_slice(outgoing, pieces, (first_dest, jnp.int32(0), jnp.int32(0)))
    incoming = lax.all_to_all(outgoing, "dp", split_axis=0, concat_axis=0, tiled=True)
    selector = (
        (col_dest[:, None] == jnp.arange(CB, dtype=jnp.int32)[None, :]) & left_dest[:, None]
    ).astype(jnp.bfloat16)
    update = jnp.einsum("srb,sc->rcb", incoming, selector, preferred_element_type=jnp.float32)
    update = update.reshape(dest_rows, CB * B).astype(jnp.bfloat16)
    return (update, root, graft)


def solution(mesh):
    return jax.shard_map(
        on_device,
        mesh=mesh,
        in_specs=(P("dp", None), P("dp", "mp"), P()),
        out_specs=(P("dp", "mp"), P("dp", "mp"), P()),
        check_vma=False,
    )
```

profile of v0, /device:TPU:0, one launch (start us, length us, event | category | flops | bytes accessed | tf_op | source)
XLA Modules:
  0.0 190.2 jit_solution(12887503934430091397)
XLA Ops:
  1.6 1.1 copy.24
  2.9 0.8 copy-done.3
  5.5 32.8 %all_to_all.20 = bf16[128,8,512]{2,0,1:T(8,128)(2,1)S(1)} all-to-all(bf16[128,8,512]{2,0,1:T(8,128)(2,1)S(1)} %bitcast_select_fusion.1), channel_id=1, replica_groups=mesh['dp'=8,'mp'=4] {'dp'}, dimensions={1} | all-to-all | bytes 2097152 | tf_op jit(solution)/shard_map/all_to_all | solution.py:70
  38.3 1.4 collective-permute-start
  41.0 21.1 %collective-permute-done = bf16[1024,512]{1,0:T(8,128)(2,1)S(1)} collective-permute-done((bf16[1024,512]{1,0:T(8,128)(2,1)S(1)}, bf16[1024,512]{1,0:T(8,128)(2,1)S(1)}, u32[]{:S(2)}, u32[]{:S(2)}) %collective-permute-start) | collective-permute-done | bytes 1048608 | tf_op jit(solution)/shard_map/ppermute | solution.py:14
  62.1 1.4 convolution_multiply_fusion
  63.8 1.6 select_reduce_fusion.1
  66.0 3.3 %multiply_reduce_fusion = (f32[]{:T(128)}, f32[512,512]{1,0:T(8,128)S(1)}) fusion(f32[]{:T(128)S(6)} %mul_shard_map.3, f32[512,512]{1,0:T(8,128)S(1)} %convolution_multiply_fusion, f32[512,512]{0,1:T(8,128)S(1)} %copy.26, pred[]{:T(512)} %bitcast.1), kind=kOutput, calls=%fused_computation.23 | convolution fusion | flops 1612185600 | bytes 3145737 | tf_op jit(solution)/shard_map/dot_general | solution.py:18
  70.0 2.0 %fusion.7 = f32[512,512]{1,0:T(8,128)S(1)} fusion(f32[512,512]{1,0:T(8,128)S(1)} %get-tuple-element.15, f32[]{:T(128)S(6)} %sqrt.6), kind=kOutput, calls=%fused_computation.19 | convolution fusion | flops 1611923456 | bytes 2097156 | tf_op jit(solution)/shard_map/dot_general | solution.py:18
  72.0 1.8 fusion.51
  73.8 1.9 fusion.50
  75.7 1.9 %fusion.14 = f32[512,512]{1,0:T(8,128)S(1)} fusion(f32[512,512]{1,0:T(8,128)S(1)} %fusion.50), kind=kOutput, calls=%fused_computation.30 | convolution fusion | flops 1611661312 | bytes 2097152 | tf_op jit(solution)/shard_map/dot_general | solution.py:18
  77.6 1.8 fusion.52
  79.5 2.0 %fusion = f32[512,512]{1,0:T(8,128)S(1)} fusion(f32[512,512]{1,0:T(8,128)S(1)} %fusion.52, f32[512,512]{1,0:T(8,128)S(1)} %fusion.50), kind=kOutput, calls=%fused_computation.7 | convolution fusion | flops 1611661312 | bytes 3145728 | tf_op jit(solution)/shard_map/dot_general | solution.py:18
  81.6 3.5 %fusion.9 = f32[512,512]{1,0:T(8,128)S(1)} fusion(f32[512,512]{1,0:T(8,128)} %copy-done.1, f32[]{:T(128)S(6)} %mul.63, f32[512,512]{1,0:T(8,128)} %copy-done.2, f32[]{:T(128)S(6)} %sqrt.6), kind=kOutput, calls=%fused_computation.21 | convolution fusion | flops 1612972032 | bytes 3145736 | tf_op jit(solution)/shard_map/dot_general | solution.py:18
  85.2 1.8 fusion.53
  87.0 1.6 collective-permute-start.1
  91.8 18.1 %collective-permute-done.1 = f32[512,512]{1,0:T(8,128)S(1)} collective-permute-done((f32[512,512]{1,0:T(8,128)S(1)}, f32[512,512]{1,0:T(8,128)S(1)}, u32[]{:S(2)}, u32[]{:S(2)}) %collective-permute-start.1) | collective-permute-done | bytes 1048608 | tf_op jit(solution)/shard_map/ppermute | solution.py:14
  110.0 2.5 %fusion.3 = f32[512,512]{1,0:T(8,128)S(1)} fusion(f32[512,512]{1,0:T(8,128)S(1)} %convolution_multiply_fusion, f32[512,512]{1,0:T(8,128)S(1)} %collective-permute-done.1, f32[512,512]{1,0:T(8,128)S(1)} %fusion.53, pred[]{:T(512)} %bitcast.1), kind=kOutput, calls=%fused_computation.15 | convolution fusion | flops 1610874880 | bytes 4194305 | tf_op jit(solution)/shard_map/dot_general | solution.py:18
  112.5 2.5 %select_reduce_fusion = (f32[512]{0:T(512)S(1)}, f32[512,512]{1,0:T(8,128)S(1)}) fusion(pred[512]{0:T(512)(128)(4,1)S(1)} %fusion.31, f32[512,512]{1,0:T(8,128)S(1)} %fusion.3, f32[512,512]{1,0:T(8,128)S(1)} %fusion.53, f32[512,512]{1,0:T(8,128)S(1)} %collective-permute-done.1, pred[]{:T(512)} %bitcast.1), kind=kOutput, calls=%fused_computation.14 | convolution fusion | flops 1611660800 | bytes 4196865 | tf_op jit(solution)/shard_map/dot_general | solution.py:18
  115.0 39.3 %all-reduce = (f32[512]{0:T(512)S(1)}, f32[512]{0:T(512)S(1)}) all-reduce(f32[512]{0:T(512)S(1)} %get-tuple-element.4, f32[512]{0:T(512)S(1)} %get-tuple-element.16), channel_id=1, replica_groups=mesh['dp'=8,'mp'=4] {'dp','mp'}, use_global_device_ids=true, to_apply=%region_3.5 | all-reduce | flops 1024 | bytes 8192 | tf_op jit(solution)/shard_map/psum | solution.py:79
  156.9 0.8 select_convert_fusion
  157.8 29.7 %all_to_all.21 = bf16[8,128,512]{2,1,0:T(8,128)(2,1)S(1)} all-to-all(bf16[8,128,512]{2,1,0:T(8,128)(2,1)S(1)} %constant_dynamic-update-slice_fusion), channel_id=1, replica_groups=mesh['dp'=8,'mp'=4] {'dp'}, dimensions={0} | all-to-all | bytes 2097152 | tf_op jit(solution)/shard_map/all_to_all | solution.py:95
  187.6 0.7 convolution_convert_fusion
  (31 shorter events, 7.1 us)
Async XLA Ops:
  0.6 0.7 copy-start.4
  2.7 1.0 copy-start.3
  38.3 23.7 %collective-permute-start = (bf16[1024,512]{1,0:T(8,128)(2,1)S(1)}, bf16[1024,512]{1,0:T(8,128)(2,1)S(1)}, u32[]{:S(2)}, u32[]{:S(2)}) collective-permute-start(bf16[1024,512]{1,0:T(8,128)(2,1)S(1)} %bitcast.39), channel_id=1, source_target_pairs={{0,4},{4,0},{8,12},{12,8},{16,20},{20,16},{24,28},{28,24},{1,5},{5... | collective-permute-start | bytes 3145736 | tf_op jit(solution)/shard_map/ppermute | solution.py:14
  69.3 4.5 %copy-start.2 = (f32[512,512]{1,0:T(8,128)}, f32[512,512]{1,0:T(8,128)S(1)}, u32[]{:S(2)}) copy-start(f32[512,512]{1,0:T(8,128)S(1)} %get-tuple-element.15) | copy-start | bytes 3145732
  75.7 3.8 %copy-start.1 = (f32[512,512]{1,0:T(8,128)}, f32[512,512]{1,0:T(8,128)S(1)}, u32[]{:S(2)}) copy-start(f32[512,512]{1,0:T(8,128)S(1)} %fusion.50) | copy-start | bytes 3145732
  87.0 25.5 %copy-start = (f32[512,512]{1,0:T(8,128)}, f32[512,512]{1,0:T(8,128)S(1)}, u32[]{:S(2)}) copy-start(f32[512,512]{1,0:T(8,128)S(1)} %fusion.53) | copy-start | bytes 3145732
  87.0 22.9 %collective-permute-start.1 = (f32[512,512]{1,0:T(8,128)S(1)}, f32[512,512]{1,0:T(8,128)S(1)}, u32[]{:S(2)}, u32[]{:S(2)}) collective-permute-start(f32[512,512]{1,0:T(8,128)S(1)} %fusion.53), channel_id=1, source_target_pairs={{0,4},{4,0},{8,12},{12,8},{16,20},{20,16},{24,28},{28,24},{1,5},{5... | collective-permute-start | bytes 3145736 | tf_op jit(solution)/shard_map/ppermute | solution.py:14
where the time goes:
time: 191 us; the launch traced here: 190 us
  blocking collectives  102 us (53%)
  waiting for transfers between devices  39.2 us (21%)
  matrix products  27.3 us (14%)
  between operations  7.38 us (4%)
  local copies, waits for them, and re-layouts  5.98 us (3%)
  other arithmetic  5.36 us (3%)
  starting transfers between devices  3.01 us (2%)
    psum x1, blocking collectives, on_device(): grad_total = jnp.sum(lax.psum(grad_share, ('dp', 'mp')))  39.3 us
    ppermute x2, waiting for transfers between devices, partner_2(): lax.ppermute(value, axis, [(i, i ^ 1 << bit) for i in range(lax.axis_size...  39.2 us
    all_to_all x1, blocking collectives, on_device(): lax.all_to_all(mixed, 'dp', split_axis=1, concat_axis=0, tiled=True)  32.8 us
    all_to_all x1, blocking collectives, on_device(): lax.all_to_all(outgoing, 'dp', split_axis=0, concat_axis=0, tiled=True)  29.7 us
    dot_general x11, matrix products, product(): jnp.dot(left, right, precision=lax.Precision.HIGHEST, preferred_element_t...  25.2 us
  transfers between devices with their start and end apart: 2, of which 2 were waited for; matrix products, arithmetic and copies ran while one was open for 1% of the time, Pallas kernels for 0%

commit v1 on v0

v1 whole, which is shorter than its diff:
```python
import functools
import math

import jax
import jax.numpy as jnp
from jax import lax
from jax.experimental import pallas as pl
from jax.experimental.pallas import tpu as pltpu
from jax.sharding import PartitionSpec as P

B = 512
CB = 2
MESH = pl.DeviceIdType.MESH


def gather_kernel(dp, mp, a_sel, c_sel, a_all, c_all, az_send, ax_send, am_send, cz_send, cx_send, a_recv, c_recv):
    pairs = dp // 2
    me = lax.axis_index("dp")
    col = lax.axis_index("mp")
    pair = me // 2
    side = me % 2
    across = 2 * pair + 1 - side

    def source(k):
        return 2 * lax.rem(pair + k, pairs) + side

    barrier = pltpu.get_barrier_semaphore()
    for k in range(1, pairs):
        pl.semaphore_signal(barrier, inc=1, device_id=(source(k), col), device_id_type=MESH)
    pl.semaphore_signal(barrier, inc=1, device_id=(across, col), device_id_type=MESH)
    for k in range(1, mp):
        pl.semaphore_signal(barrier, inc=1, device_id=(me, lax.rem(col + k, mp)), device_id_type=MESH)
    pl.semaphore_wait(barrier, pairs - 1 + 1 + mp - 1)

    def a_pair(k):
        dest = lax.rem(pair + k, pairs)
        return pltpu.make_async_remote_copy(
            a_sel.at[dest], a_all.at[me, col], az_send.at[k], a_recv.at[me, col], (source(k), col), MESH)

    def c_pair(k):
        dest = lax.rem(pair + k, pairs)
        return pltpu.make_async_remote_copy(
            c_sel.at[dest], c_all.at[me], cz_send.at[k], c_recv.at[me], (source(k), col), MESH)

    def a_across(k):
        src = source(k)
        ref = a_sel.at[pair] if k == 0 else a_all.at[src, col]
        return pltpu.make_async_remote_copy(
            ref, a_all.at[src, col], ax_send.at[k], a_recv.at[src, col], (across, col), MESH)

    def c_across(k):
        src = source(k)
        ref = c_sel.at[pair] if k == 0 else c_all.at[src]
        return pltpu.make_async_remote_copy(
            ref, c_all.at[src], cx_send.at[k], c_recv.at[src], (across, col), MESH)

    def a_mp(src, k, own=False):
        ref = a_sel.at[pair] if own else a_all.at[src, col]
        return pltpu.make_async_remote_copy(
            ref, a_all.at[src, col], am_send.at[src, k], a_recv.at[src, col], (me, lax.rem(col + k, mp)), MESH)

    def start_mp(src):
        @pl.loop(1, mp)
        def _(k):
            a_mp(src, k).start()

    def a_arrived(src, who):
        pltpu.make_async_copy(a_all.at[src, who], a_all.at[src, who], a_recv.at[src, who]).wait()

    def c_arrived(src):
        pltpu.make_async_copy(c_all.at[src], c_all.at[src], c_recv.at[src]).wait()

    order = list(range(1, pairs))
    a_across(0).start()
    for k in order:
        a_pair(k).start()
    c_across(0).start()
    for k in order:
        c_pair(k).start()

    @pl.loop(1, mp)
    def _(k):
        a_mp(me, k, own=True).start()

    a_all[me, col] = a_sel[pair]
    c_all[me] = c_sel[pair]
    for k in order:
        a_arrived(source(k), col)
        a_across(k).start()
        start_mp(source(k))
    for k in range(pairs):
        other = source(k) + 1 - 2 * side
        a_arrived(other, col)
        start_mp(other)
    for k in order:
        c_arrived(source(k))
        c_across(k).start()

    @pl.loop(0, dp)
    def _(src):
        @pl.loop(1, mp)
        def _(k):
            a_arrived(src, lax.rem(col + k, mp))
            a_mp(src, k).wait_send()

    for k in range(pairs):
        c_arrived(source(k) + 1 - 2 * side)
    for k in range(pairs):
        a_across(k).wait_send()
        c_across(k).wait_send()
    for k in order:
        a_pair(k).wait_send()
        c_pair(k).wait_send()


def finish_kernel(dp, mp, owners, stats, pre, update, graft_ref, slots, out, got, m_send, m_recv, d_send, d_recv, u_send, u_recv):
    pairs = dp // 2
    halves = pre.shape[0]
    me = lax.axis_index("dp")
    col = lax.axis_index("mp")
    pair = me // 2
    side = me % 2

    barrier = pltpu.get_barrier_semaphore()
    for k in range(1, dp):
        pl.semaphore_signal(barrier, inc=1, device_id=(lax.rem(me + k, dp), col), device_id_type=MESH)
    for k in range(1, mp):
        pl.semaphore_signal(barrier, inc=1, device_id=(me, lax.rem(col + k, mp)), device_id_type=MESH)
    slots[me, col] = stats[...]
    pl.semaphore_wait(barrier, dp - 1 + mp - 1)

    def over_mp(k):
        return pltpu.make_async_remote_copy(
            stats, slots.at[me, col], m_send.at[k], m_recv.at[col], (me, lax.rem(col + k, mp)), MESH)

    def over_dp(k):
        return pltpu.make_async_remote_copy(
            slots.at[me], slots.at[me], d_send.at[k], d_recv.at[me], (lax.rem(me + k, dp), col), MESH)

    for k in range(1, mp):
        over_mp(k).start()
    for k in range(1, mp):
        who = lax.rem(col + k, mp)
        pltpu.make_async_copy(stats, stats, m_recv.at[who]).wait()
    for k in range(1, dp):
        over_dp(k).start()
    for k in range(1, dp):
        who = lax.rem(me + k, dp)
        pltpu.make_async_copy(slots.at[who], slots.at[who], d_recv.at[who]).wait()
    totals = jnp.sum(slots[...].reshape(dp * mp, *stats.shape), axis=0)
    grad_total = totals[0:1, 0:1]
    pre_total = totals[1:2, 0:1]
    graft = jnp.sqrt(grad_total / jnp.maximum(pre_total, 1.0))
    graft_ref[...] = jnp.broadcast_to(graft, graft_ref.shape)
    out[...] = (pre[...] * graft[None]).astype(jnp.bfloat16)

    def piece(k):
        dest = lax.rem(pair + k, pairs)
        return pltpu.make_async_remote_copy(
            out.at[dest % halves], got.at[pair], u_send.at[k], u_recv.at[pair], (2 * dest + side, col), MESH)

    for k in range(1, pairs):
        piece(k).start()
    got[pair] = out[pair % halves]
    for k in range(1, pairs):
        who = lax.rem(pair + k, pairs)
        pltpu.make_async_copy(got.at[who], got.at[who], u_recv.at[who]).wait()
    for c in range(CB):
        holder = owners[(pair // halves) * CB + c] // 2
        update[:, c * B : (c + 1) * B] = got[holder]
    for k in range(1, mp):
        over_mp(k).wait_send()
    for k in range(1, dp):
        over_dp(k).wait_send()
    for k in range(1, pairs):
        piece(k).wait_send()


def product(left, right):
    return jnp.matmul(left, right, precision=lax.Precision.HIGH, preferred_element_type=jnp.float32)


def inverse_roots(stat):
    eye = jnp.eye(B, dtype=jnp.float32)
    size = jnp.sqrt(jnp.sum(stat * stat))
    m = stat / size
    m2 = product(m, m)
    f = (5.0 * eye - m) * 0.25
    f2 = (25.0 * eye - 10.0 * m + m2) * 0.0625
    mf = (5.0 * m - m2) * 0.25
    y = (5.0 * f - product(product(f2, f2), mf)) * 0.25
    my = product(m, y)
    y2 = product(y, y)
    return (5.0 * y - product(product(y2, y2), my)) * (0.25 * size ** (-0.25))


def on_device(activations, cotangents, owners):
    dp = lax.axis_size("dp")
    mp = lax.axis_size("mp")
    me = lax.axis_index("dp")
    col = lax.axis_index("mp")
    pairs = dp // 2
    tokens, features = activations.shape
    part = tokens // mp
    ids = jnp.arange(owners.shape[0], dtype=jnp.int32)
    pair_ids = jnp.arange(pairs, dtype=jnp.int32)
    block_of = jnp.sum(jnp.where(owners[None, :] // 2 == pair_ids[:, None], ids[None, :], 0), axis=1)
    my_block = block_of[me // 2]
    my_left = owners[my_block] == me

    mine = lax.dynamic_slice_in_dim(activations, col * part, part, 0)
    a_sel = jnp.take(mine.reshape(part, features // B, B).transpose(1, 0, 2), block_of // CB, axis=0)
    c_sel = jnp.take(cotangents.reshape(tokens, CB, B).transpose(1, 0, 2), block_of % CB, axis=0)
    vmem = pl.BlockSpec(memory_space=pltpu.VMEM)
    dma = pltpu.SemaphoreType.DMA
    a_all, c_all = pl.pallas_call(
        functools.partial(gather_kernel, dp, mp),
        out_shape=(
            jax.ShapeDtypeStruct((dp, mp, part, B), jnp.bfloat16),
            jax.ShapeDtypeStruct((dp, tokens, B), jnp.bfloat16),
        ),
        in_specs=[vmem] * 2,
        out_specs=(vmem, vmem),
        scratch_shapes=[
            dma((pairs,)), dma((pairs,)), dma((dp, mp)), dma((pairs,)), dma((pairs,)), dma((dp, mp)), dma((dp,)),
        ],
        compiler_params=pltpu.CompilerParams(collective_id=0, has_side_effects=True),
    )(a_sel, c_sel)

    all_tokens = dp * tokens
    gradient = lax.dot_general(
        a_all.reshape(all_tokens, B), c_all.reshape(all_tokens, B), (((0,), (0,)), ((), ())),
        preferred_element_type=jnp.float32,
    ) / math.sqrt(all_tokens)
    ridge = 0.1 * (jnp.sum(gradient * gradient) / B + 1.0) * jnp.eye(B, dtype=jnp.float32)
    left = inverse_roots(product(gradient, gradient.T) + ridge)
    right = inverse_roots(product(gradient.T, gradient) + ridge)
    root = jnp.where(my_left, left, right)

    rows = features // dp
    halves = B // rows // 2

    def my_rows(matrix):
        return lax.dynamic_index_in_dim(matrix.reshape(halves, 2, rows, B), me % 2, 1, keepdims=False)

    pre = product(product(my_rows(left).reshape(halves * rows, B), gradient), right)
    sums = jnp.stack([jnp.sum(jnp.square(my_rows(gradient))), jnp.sum(pre * pre)])
    stats = jnp.zeros((8, 128), jnp.float32).at[0:2, :].set(sums[:, None])
    update, graft = pl.pallas_call(
        functools.partial(finish_kernel, dp, mp),
        out_shape=(
            jax.ShapeDtypeStruct((rows, CB * B), jnp.bfloat16),
            jax.ShapeDtypeStruct((8, 128), jnp.float32),
        ),
        in_specs=[pl.BlockSpec(memory_space=pltpu.SMEM), vmem, vmem],
        out_specs=(vmem, vmem),
        scratch_shapes=[
            pltpu.VMEM((dp, mp, 8, 128), jnp.float32),
            pltpu.VMEM((halves, rows, B), jnp.bfloat16),
            pltpu.VMEM((pairs, rows, B), jnp.bfloat16),
            dma((mp,)), dma((mp,)), dma((dp,)), dma((dp,)), dma((pairs,)), dma((pairs,)),
        ],
        compiler_params=pltpu.CompilerParams(collective_id=1, has_side_effects=True),
    )(owners, stats, pre.reshape(halves, rows, B))
    return (update, root, graft[0, 0])


def solution(mesh):
    return jax.shard_map(
        on_device,
        mesh=mesh,
        in_specs=(P("dp", None), P("dp", "mp"), P()),
        out_specs=(P("dp", "mp"), P("dp", "mp"), P()),
        check_vma=False,
    )
```

time: 191 us -> 97.8 us (0.51)
  blocking collectives: 102 us -> 0 us
  Pallas kernels: 0 us -> 55.7 us
  waiting for transfers between devices: 39.2 us -> 0 us
  starting transfers between devices: 3.01 us -> 0 us
  matrix products: 27.3 us -> 25.3 us
    all_to_all x2 -> x0, blocking collectives: 62.6 us -> none  [the longest x1 32.8 us: on_device(): lax.all_to_all(mixed, 'dp', split_axis=1, concat_axis=0, tiled=True)]
    pallas_call x0 -> x2, Pallas kernels: none -> 55.7 us  [the longest x1 28.5 us: on_device(): pl.pallas_call(functools.partial(gather_kernel, dp, mp), out_shape=(jax.S...]
    psum x1 -> x0, blocking collectives: 39.3 us -> none  [on_device(): grad_total = jnp.sum(lax.psum(grad_share, ('dp', 'mp')))]
    ppermute x2 -> x0, waiting for transfers between devices: 39.2 us -> none  [partner_2(): lax.ppermute(value, axis, [(i, i ^ 1 << bit) for i in range(lax.axis_size...]
    ppermute x2 -> x0, starting transfers between devices: 3.01 us -> none  [partner_2(): lax.ppermute(value, axis, [(i, i ^ 1 << bit) for i in range(lax.axis_size...]
    dot_general x13 -> x19, matrix products: 27.3 us -> 25.3 us  [the longest x18 22.3 us: product(): jnp.matmul(left, right, precision=lax.Precision.HIGH, preferred_element_t...]
    reduce_sum x4 -> x2, other arithmetic: 2.86 us -> 0.86 us  [the longest x1 0.74 us: on_device(): jnp.sum(jnp.square(my_rows(gradient)))]
  transfers between devices with their start and end apart: 2 -> 0, of which waited for: 2 -> 0; matrix products, arithmetic and copies ran while one was open for 1% -> 0% of each run, Pallas kernels for 0% -> 0%
where the time goes in v1:
time: 97.8 us; the launch traced here: 97.5 us
  Pallas kernels  55.7 us (57%)
  matrix products  25.3 us (26%)
  local copies, waits for them, and re-layouts  6.9 us (7%)
  between operations  5.63 us (6%)
  other arithmetic  3.91 us (4%)
    pallas_call x1, Pallas kernels, on_device(): pl.pallas_call(functools.partial(gather_kernel, dp, mp), out_shape=(jax.S...  28.5 us
    pallas_call x1, Pallas kernels, on_device(): pl.pallas_call(functools.partial(finish_kernel, dp, mp), out_shape=(jax.S...  27.2 us
    dot_general x18, matrix products, product(): jnp.matmul(left, right, precision=lax.Precision.HIGH, preferred_element_t...  22.3 us
    dot_general x1, matrix products, on_device(): lax.dot_general(a_all.reshape(all_tokens, B), c_all.reshape(all_tokens, B...  3.03 us
    unnamed x8, local copies, waits for them, and re-layouts  2.54 us

profile of v1, /device:TPU:0, one launch (start us, length us, event | category | flops | bytes accessed | tf_op | source)
XLA Modules:
  0.0 97.5 jit_solution(18340472802795726218)
XLA Ops:
  7.6 0.9 broadcast_select_fusion.c_sel
  8.5 28.5 %shard_map.58 = (bf16[8,4,32,512]{3,2,1,0:T(8,128)(2,1)}, bf16[8,128,512]{2,1,0:T(8,128)(2,1)}) custom-call(bf16[4,32,512]{2,1,0:T(8,128)(2,1)} %broadcast_select_fusion.2.a_sel, bf16[4,128,512]{2,1,0:T(8,128)(2,1)} %broadcast_select_fusion.c_sel), custom_call_target="tpu_custom_call" | custom-call | tf_op jit(solution)/shard_map/pallas_call | solution.py:216
  37.0 3.0 %multiply_reduce_fusion.2 = (f32[]{:T(128)}, f32[512,512]{1,0:T(8,128)S(1)}) fusion(bf16[1024,512]{1,0:T(8,128)(2,1)} %bitcast.69, bf16[1024,512]{1,0:T(8,128)(2,1)} %bitcast.70), kind=kOutput, calls=%fused_computation.33 | convolution fusion | flops 537657344 | bytes 3145732 | tf_op jit(solution)/shard_map/dot_general | solution.py:231
  41.4 1.8 %multiply_reduce_fusion = (f32[]{:T(128)}, f32[512,512]{1,0:T(8,128)S(1)}) fusion(f32[]{:T(128)S(6)} %mul_shard_map.3, f32[512,512]{1,0:T(8,128)S(1)} %get-tuple-element.28), kind=kOutput, calls=%fused_computation.27 | convolution fusion | flops 806617088 | bytes 2097160 | tf_op jit(solution)/shard_map/dot_general | solution.py:180
  44.0 1.0 %fusion.64 = f32[512,512]{1,0:T(8,128)S(1)} fusion(f32[512,512]{1,0:T(8,128)S(1)} %get-tuple-element.32, f32[]{:T(128)S(6)} %sqrt.7), kind=kOutput, calls=%fused_computation.116 | convolution fusion | flops 805568512 | bytes 2097156 | tf_op jit(solution)/shard_map/dot_general | solution.py:180
  45.0 1.2 %fusion.10 = f32[512,512]{1,0:T(8,128)S(1)} fusion(f32[512,512]{1,0:T(8,128)S(1)} %fusion.64, f32[512,512]{1,0:T(8,128)S(1)} %get-tuple-element.32, f32[]{:T(128)S(6)} %sqrt.7), kind=kOutput, calls=%fused_computation.22 | convolution fusion | flops 807141376 | bytes 3145732 | tf_op jit(solution)/shard_map/dot_general | solution.py:180
  46.2 1.1 %convolution_subtract_fusion.1 = f32[512,512]{1,0:T(8,128)S(1)} fusion(f32[512,512]{1,0:T(8,128)S(1)} %fusion.10, f32[512,512]{1,0:T(8,128)S(1)} %fusion.64, f32[512,512]{1,0:T(8,128)S(1)} %get-tuple-element.32, f32[]{:T(128)S(6)} %sqrt.7), kind=kOutput, calls=%fused_computation.10 | convolution fusion | flops 807927808 | bytes 4194308 | tf_op jit(solution)/shard_map/dot_general | solution.py:180
  47.3 1.0 %fusion.20 = f32[512,512]{1,0:T(8,128)S(1)} fusion(f32[512,512]{1,0:T(8,128)S(1)} %convolution_subtract_fusion.1, f32[512,512]{1,0:T(8,128)S(1)} %get-tuple-element.32, f32[]{:T(128)S(6)} %sqrt.7), kind=kOutput, calls=%fused_computation.35 | convolution fusion | flops 805830656 | bytes 3145732 | tf_op jit(solution)/shard_map/dot_general | solution.py:180
  48.3 1.0 %fusion.22 = f32[512,512]{1,0:T(8,128)S(1)} fusion(f32[512,512]{1,0:T(8,128)S(1)} %convolution_subtract_fusion.1), kind=kOutput, calls=%fused_computation.37 | convolution fusion | flops 805568512 | bytes 2097152 | tf_op jit(solution)/shard_map/dot_general | solution.py:180
  49.4 1.0 %fusion.67 = f32[512,512]{1,0:T(8,128)S(1)} fusion(f32[512,512]{1,0:T(8,128)S(1)} %fusion.22), kind=kOutput, calls=%fused_computation.119 | convolution fusion | flops 805306368 | bytes 2097152 | tf_op jit(solution)/shard_map/dot_general | solution.py:180
  50.4 1.0 %fusion = f32[512,512]{1,0:T(8,128)S(1)} fusion(f32[512,512]{1,0:T(8,128)S(1)} %fusion.67, f32[512,512]{1,0:T(8,128)S(1)} %fusion.20, f32[512,512]{1,0:T(8,128)S(1)} %convolution_subtract_fusion.1, f32[]{:T(128)S(6)} %mul.123), kind=kOutput, calls=%fused_computation.9 | convolution fusion | flops 806092800 | bytes 4194308 | tf_op jit(solution)/shard_map/dot_general | solution.py:180
  51.4 1.8 %multiply_reduce_fusion.1 = (f32[]{:T(128)}, f32[512,512]{1,0:T(8,128)S(1)}) fusion(f32[]{:T(128)S(6)} %mul_shard_map.3, f32[512,512]{1,0:T(8,128)S(1)} %get-tuple-element.28), kind=kOutput, calls=%fused_computation.32 | convolution fusion | flops 806617088 | bytes 2097160 | tf_op jit(solution)/shard_map/dot_general | solution.py:180
  53.9 1.0 %fusion.63 = f32[512,512]{1,0:T(8,128)S(1)} fusion(f32[512,512]{1,0:T(8,128)S(1)} %get-tuple-element.30, f32[]{:T(128)S(6)} %sqrt.6), kind=kOutput, calls=%fused_computation.115 | convolution fusion | flops 805568512 | bytes 2097156 | tf_op jit(solution)/shard_map/dot_general | solution.py:180
  54.9 1.4 %fusion.6 = f32[512,512]{1,0:T(8,128)S(1)} fusion(f32[512,512]{1,0:T(8,128)S(1)} %fusion.63, f32[512,512]{1,0:T(8,128)S(1)} %get-tuple-element.30, f32[]{:T(128)S(6)} %sqrt.6), kind=kOutput, calls=%fused_computation.19 | convolution fusion | flops 807141376 | bytes 3145732 | tf_op jit(solution)/shard_map/dot_general | solution.py:180
  56.3 1.1 %convolution_subtract_fusion.3 = f32[512,512]{1,0:T(8,128)S(1)} fusion(f32[512,512]{1,0:T(8,128)S(1)} %fusion.6, f32[512,512]{1,0:T(8,128)S(1)} %fusion.63, f32[512,512]{1,0:T(8,128)S(1)} %get-tuple-element.30, f32[]{:T(128)S(6)} %sqrt.6), kind=kOutput, calls=%fused_computation.13 | convolution fusion | flops 807927808 | bytes 4194308 | tf_op jit(solution)/shard_map/dot_general | solution.py:180
  57.5 1.0 %fusion.24 = f32[512,512]{1,0:T(8,128)S(1)} fusion(f32[512,512]{1,0:T(8,128)S(1)} %convolution_subtract_fusion.3, f32[512,512]{1,0:T(8,128)S(1)} %get-tuple-element.30, f32[]{:T(128)S(6)} %sqrt.6), kind=kOutput, calls=%fused_computation.39 | convolution fusion | flops 805830656 | bytes 3145732 | tf_op jit(solution)/shard_map/dot_general | solution.py:180
  58.5 1.1 %fusion.26 = f32[512,512]{1,0:T(8,128)S(1)} fusion(f32[512,512]{1,0:T(8,128)S(1)} %convolution_subtract_fusion.3), kind=kOutput, calls=%fused_computation.41 | convolution fusion | flops 805568512 | bytes 2097152 | tf_op jit(solution)/shard_map/dot_general | solution.py:180
  59.6 1.0 %fusion.65 = f32[512,512]{1,0:T(8,128)S(1)} fusion(f32[512,512]{1,0:T(8,128)S(1)} %fusion.26), kind=kOutput, calls=%fused_computation.117 | convolution fusion | flops 805306368 | bytes 2097152 | tf_op jit(solution)/shard_map/dot_general | solution.py:180
  60.6 2.1 %broadcast_select_fusion.1 = (f32[512,512]{1,0:T(8,128)}, f32[512,512]{1,0:T(8,128)S(1)}) fusion(f32[512,512]{1,0:T(8,128)S(1)} %fusion, pred[]{:T(512)S(6)} %eq.38, f32[]{:T(128)S(6)} %mul.112, f32[512,512]{1,0:T(8,128)S(1)} %fusion.65, f32[512,512]{1,0:T(8,128)S(1)} %fusion.24, f32[512,512]{1,0:T(8,128)S(1)} %convolution_subtract_fusion.3), kind=kOutput, calls=%fused_computation.64 | convolution fusion | flops 806354944 | bytes 6291461 | tf_op jit(solution)/shard_map/dot_general | solution.py:180
  63.3 2.0 %multiply_reduce_fusion.3 = (f32[]{:T(128)}, f32[256,512]{1,0:T(8,128)}) fusion(f32[256,512]{1,0:T(8,128)S(1)} %fusion.66, f32[512,512]{1,0:T(8,128)S(1)} %fusion), kind=kOutput, calls=%fused_computation.43 | convolution fusion | flops 402915328 | bytes 2097156 | tf_op jit(solution)/shard_map/dot_general | solution.py:180
  65.4 1.4 %fusion.44 = f32[8]{0:T(128)S(1)} fusion(f32[1]{0:T(128)} %bitcast.12, f32[1]{0:T(128)} %bitcast.9), kind=kLoop, calls=%fused_computation.95 | loop fusion | flops 32 | bytes 40 | tf_op jit(solution)/shard_map/stack | solution.py:247
  67.4 27.2 %shard_map.59 = (bf16[128,1024]{1,0:T(8,128)(2,1)}, f32[8,128]{1,0:T(8,128)}) custom-call(s32[4]{0:T(128)} %owners.1, f32[8,128]{1,0:T(8,128)} %scatter.8.stats, f32[2,128,512]{2,1,0:T(8,128)} %bitcast.64), custom_call_target="tpu_custom_call" | custom-call | tf_op jit(solution)/shard_map/pallas_call | solution.py:249
  94.6 1.2 %slice.19 = f32[1,1]{1,0:T(1,128)} slice(f32[8,128]{1,0:T(8,128)} %get-tuple-element.22), slice={[0:1], [0:1]} | slice | bytes 8 | tf_op jit(solution)/shard_map/slice | solution.py:265
  95.8 1.7 %copy.16 = bf16[128,1024]{1,0:T(8,128)(2,1)} copy(bf16[128,1024]{1,0:T(8,128)(2,1)} %get-tuple-element.42) | data formatting | bytes 524288
  (24 shorter events, 6.3 us)
Async XLA Ops:
  0.6 4.7 %copy-start = (bf16[128,1024]{1,0:T(8,128)(2,1)S(1)}, bf16[128,1024]{1,0:T(8,128)(2,1)}, u32[]{:S(2)}) copy-start(bf16[128,1024]{1,0:T(8,128)(2,1)} %param.5) | copy-start | bytes 786436
  0.7 0.7 copy-start.2
  5.4 1.3 %copy-start.1 = (bf16[128,1024]{1,0:T(8,128)(2,1)S(1)}, bf16[128,1024]{1,0:T(8,128)(2,1)}, u32[]{:S(2)}) copy-start(bf16[128,1024]{1,0:T(8,128)(2,1)} %param.6) | copy-start | bytes 786436

commit v2 on v1

--- a/solution.py
+++ b/solution.py
@@ -13,7 +13,7 @@
 MESH = pl.DeviceIdType.MESH
 
 
-def gather_kernel(dp, mp, a_sel, c_sel, a_all, c_all, az_send, ax_send, am_send, cz_send, cx_send, a_recv, c_recv):
+def gather_kernel(dp, mp, owners, acts, cots, grad, oriented, a_sel, c_sel, a_all, c_all, az_send, ax_send, am_send, cz_send, cx_send, a_recv, c_recv):
     pairs = dp // 2
     me = lax.axis_index("dp")
     col = lax.axis_index("mp")
@@ -30,6 +30,30 @@
     pl.semaphore_signal(barrier, inc=1, device_id=(across, col), device_id_type=MESH)
     for k in range(1, mp):
         pl.semaphore_signal(barrier, inc=1, device_id=(me, lax.rem(col + k, mp)), device_id_type=MESH)
+
+    def block_of(which):
+        held = [jnp.where(owners[b] // 2 == which, b, 0) for b in range(owners.shape[0])]
+        return functools.reduce(jnp.add, held)
+
+    def chosen(wide, which):
+        parts = [
+            wide[:, n * B : (n + 1) * B] * jnp.where(which == n, 1.0, 0.0).astype(wide.dtype)
+            for n in range(wide.shape[1] // B)
+        ]
+        return functools.reduce(jnp.add, parts)
+
+    part = a_sel.shape[1]
+    scale = 1.0 / math.sqrt(dp * cots.shape[0])
+    for dest in range(pairs):
+        block = block_of(dest)
+        row_start = pl.multiple_of(col * part, part)
+        mine = acts[pl.ds(row_start, part), :]
+        a_sel[dest] = chosen(mine, block // CB)
+        c_sel[dest] = chosen(cots[...], block % CB)
+    is_left = functools.reduce(
+        jnp.add, [jnp.where(owners[b] == me, 1.0, 0.0) for b in range(owners.shape[0])])
+    a_all[me, col] = a_sel[pair]
+    c_all[me] = c_sel[pair]
     pl.semaphore_wait(barrier, pairs - 1 + 1 + mp - 1)
 
     def a_pair(k):
@@ -82,8 +106,6 @@
     def _(k):
         a_mp(me, k, own=True).start()
 
-    a_all[me, col] = a_sel[pair]
-    c_all[me] = c_sel[pair]
     for k in order:
         a_arrived(source(k), col)
         a_across(k).start()
@@ -92,19 +114,45 @@
         other = source(k) + 1 - 2 * side
         a_arrived(other, col)
         start_mp(other)
+    def a_complete(src):
+        @pl.loop(1, mp)
+        def _(k):
+            a_arrived(src, lax.rem(col + k, mp))
+
+    def accumulate(k):
+        base = 2 * lax.rem(pair + k, pairs)
+        a_complete(base)
+        a_complete(base + 1)
+        c_arrived(source(k) + 1 - 2 * side)
+        tokens = 2 * cots.shape[0]
+        a = a_all[pl.ds(base, 2)].reshape(tokens, B)
+        c = c_all[pl.ds(base, 2)].reshape(tokens, B)
+        keep = is_left.astype(a.dtype)
+        swap = (1.0 - is_left).astype(a.dtype)
+        first = a * keep + c * swap
+        second = c * keep + a * swap
+        dims = (((0,), (0,)), ((), ()))
+        add = lax.dot_general(a, c, dims, preferred_element_type=jnp.float32) * scale
+        add_oriented = lax.dot_general(first, second, dims, preferred_element_type=jnp.float32) * scale
+        if k == 0:
+            grad[...] = add
+            oriented[...] = add_oriented
+        else:
+            grad[...] += add
+            oriented[...] += add_oriented
+
     for k in order:
         c_arrived(source(k))
         c_across(k).start()
+        accumulate(k - 1)
+    accumulate(pairs - 1)
 
     @pl.loop(0, dp)
     def _(src):
         @pl.loop(1, mp)
         def _(k):
-            a_arrived(src, lax.rem(col + k, mp))
             a_mp(src, k).wait_send()
 
-    for k in range(pairs):
-        c_arrived(source(k) + 1 - 2 * side)
     for k in range(pairs):
         a_across(k).wait_send()
         c_across(k).wait_send()
@@ -151,7 +199,7 @@
     grad_total = totals[0:1, 0:1]
     pre_total = totals[1:2, 0:1]
     graft = jnp.sqrt(grad_total / jnp.maximum(pre_total, 1.0))
-    graft_ref[...] = jnp.broadcast_to(graft, graft_ref.shape)
+    graft_ref[0, 0] = graft[0, 0]
     out[...] = (pre[...] * graft[None]).astype(jnp.bfloat16)
 
     def piece(k):
@@ -180,7 +228,7 @@
     return jnp.matmul(left, right, precision=lax.Precision.HIGH, preferred_element_type=jnp.float32)
 
 
-def inverse_roots(stat):
+def inverse_root(stat):
     eye = jnp.eye(B, dtype=jnp.float32)
     size = jnp.sqrt(jnp.sum(stat * stat))
     m = stat / size
@@ -198,62 +246,53 @@
     dp = lax.axis_size("dp")
     mp = lax.axis_size("mp")
     me = lax.axis_index("dp")
-    col = lax.axis_index("mp")
     pairs = dp // 2
     tokens, features = activations.shape
     part = tokens // mp
-    ids = jnp.arange(owners.shape[0], dtype=jnp.int32)
-    pair_ids = jnp.arange(pairs, dtype=jnp.int32)
-    block_of = jnp.sum(jnp.where(owners[None, :] // 2 == pair_ids[:, None], ids[None, :], 0), axis=1)
-    my_block = block_of[me // 2]
-    my_left = owners[my_block] == me
-
-    mine = lax.dynamic_slice_in_dim(activations, col * part, part, 0)
-    a_sel = jnp.take(mine.reshape(part, features // B, B).transpose(1, 0, 2), block_of // CB, axis=0)
-    c_sel = jnp.take(cotangents.reshape(tokens, CB, B).transpose(1, 0, 2), block_of % CB, axis=0)
     vmem = pl.BlockSpec(memory_space=pltpu.VMEM)
+    smem = pl.BlockSpec(memory_space=pltpu.SMEM)
     dma = pltpu.SemaphoreType.DMA
-    a_all, c_all = pl.pallas_call(
+    square = jax.ShapeDtypeStruct((B, B), jnp.float32)
+    gradient, oriented = pl.pallas_call(
         functools.partial(gather_kernel, dp, mp),
-        out_shape=(
-            jax.ShapeDtypeStruct((dp, mp, part, B), jnp.bfloat16),
-            jax.ShapeDtypeStruct((dp, tokens, B), jnp.bfloat16),
-        ),
-        in_specs=[vmem] * 2,
+        out_shape=(square, square),
+        in_specs=[smem, vmem, vmem],
         out_specs=(vmem, vmem),
         scratch_shapes=[
+            pltpu.VMEM((pairs, part, B), jnp.bfloat16),
+            pltpu.VMEM((pairs, tokens, B), jnp.bfloat16),
+            pltpu.VMEM((dp, mp, part, B), jnp.bfloat16),
+            pltpu.VMEM((dp, tokens, B), jnp.bfloat16),
             dma((pairs,)), dma((pairs,)), dma((dp, mp)), dma((pairs,)), dma((pairs,)), dma((dp, mp)), dma((dp,)),
         ],
         compiler_params=pltpu.CompilerParams(collective_id=0, has_side_effects=True),
-    )(a_sel, c_sel)
-
-    all_tokens = dp * tokens
-    gradient = lax.dot_general(
-        a_all.reshape(all_tokens, B), c_all.reshape(all_tokens, B), (((0,), (0,)), ((), ())),
-        preferred_element_type=jnp.float32,
-    ) / math.sqrt(all_tokens)
-    ridge = 0.1 * (jnp.sum(gradient * gradient) / B + 1.0) * jnp.eye(B, dtype=jnp.float32)
-    left = inverse_roots(product(gradient, gradient.T) + ridge)
-    right = inverse_roots(product(gradient.T, gradient) + ridge)
-    root = jnp.where(my_left, left, right)
+    )(owners, activations, cotangents)
+
+    my_left = jnp.any(owners == me)
+    grad_total = jnp.sum(oriented * oriented)
+    ridge = 0.1 * (grad_total / B + 1.0) * jnp.eye(B, dtype=jnp.float32)
+    root = inverse_root(product(oriented, oriented.T) + ridge)
 
     rows = features // dp
     halves = B // rows // 2
 
     def my_rows(matrix):
-        return lax.dynamic_index_in_dim(matrix.reshape(halves, 2, rows, B), me % 2, 1, keepdims=False)
-
-    pre = product(product(my_rows(left).reshape(halves * rows, B), gradient), right)
-    sums = jnp.stack([jnp.sum(jnp.square(my_rows(gradient))), jnp.sum(pre * pre)])
-    stats = jnp.zeros((8, 128), jnp.float32).at[0:2, :].set(sums[:, None])
+        split = matrix.reshape(halves, 2, rows, B)
+        return jnp.where(me % 2 == 0, split[:, 0], split[:, 1]).reshape(halves * rows, B)
+
+    first = jnp.where(my_left, my_rows(root), my_rows(gradient))
+    last = jnp.where(my_left, gradient, root)
+    pre = product(product(first, root), last)
+    row_ids = lax.broadcasted_iota(jnp.int32, (8, 128), 0)
+    stats = jnp.where(row_ids == 0, 0.5 * grad_total, jnp.sum(pre * pre))
     update, graft = pl.pallas_call(
         functools.partial(finish_kernel, dp, mp),
         out_shape=(
             jax.ShapeDtypeStruct((rows, CB * B), jnp.bfloat16),
-            jax.ShapeDtypeStruct((8, 128), jnp.float32),
+            jax.ShapeDtypeStruct((1, 1), jnp.float32),
         ),
-        in_specs=[pl.BlockSpec(memory_space=pltpu.SMEM), vmem, vmem],
-        out_specs=(vmem, vmem),
+        in_specs=[smem, vmem, vmem],
+        out_specs=(vmem, smem),
         scratch_shapes=[
             pltpu.VMEM((dp, mp, 8, 128), jnp.float32),
             pltpu.VMEM((halves, rows, B), jnp.bfloat16),

time: 97.8 us -> 84.3 us (0.86)
  matrix products: 25.3 us -> 15.1 us
  local copies, waits for them, and re-layouts: 6.9 us -> 3.24 us
  between operations: 5.63 us -> 4.63 us
    dot_general x18 -> x10, matrix products: 22.3 us -> 15.1 us  [product(): jnp.matmul(left, right, precision=lax.Precision.HIGH, preferred_element_t...]
    dot_general x1 -> x0, matrix products: 3.03 us -> none  [on_device(): lax.dot_general(a_all.reshape(all_tokens, B), c_all.reshape(all_tokens, B...]
    pallas_call x1, Pallas kernels: 28.5 us -> 31.5 us  [on_device(): pl.pallas_call(functools.partial(gather_kernel, dp, mp), out_shape=(squar...]
    pallas_call x1, Pallas kernels: 27.2 us -> 25.1 us  [on_device(): pl.pallas_call(functools.partial(finish_kernel, dp, mp), out_shape=(jax.S...]
    another operation x1 -> x0, other arithmetic: 1.37 us -> none  [on_device(): jnp.stack([jnp.sum(jnp.square(my_rows(gradient))), jnp.sum(pre * pre)])]
    reduce_sum x2 -> x1, other arithmetic: 0.86 us -> 2.19 us  [on_device(): grad_total = jnp.sum(oriented * oriented)]
    dynamic_slice x4 -> x0, local copies, waits for them, and re-layouts: 1.22 us -> none  [the longest x1 0.59 us: on_device(): my_block = block_of[me // 2]]
    slice x1 -> x0, local copies, waits for them, and re-layouts: 1.19 us -> none  [on_device(): return (update, root, graft[0, 0])]
where the time goes in v2:
time: 84.3 us; the launch traced here: 83.9 us
  Pallas kernels  56.6 us (67%)
  matrix products  15.1 us (18%)
  between operations  4.63 us (5%)
  other arithmetic  4.37 us (5%)
  local copies, waits for them, and re-layouts  3.24 us (4%)
    pallas_call x1, Pallas kernels, on_device(): pl.pallas_call(functools.partial(gather_kernel, dp, mp), out_shape=(squar...  31.5 us
    pallas_call x1, Pallas kernels, on_device(): pl.pallas_call(functools.partial(finish_kernel, dp, mp), out_shape=(jax.S...  25.1 us
    dot_general x10, matrix products, product(): jnp.matmul(left, right, precision=lax.Precision.HIGH, preferred_element_t...  15.1 us
    unnamed x15, local copies, waits for them, and re-layouts  2.58 us
    reduce_sum x1, other arithmetic, on_device(): grad_total = jnp.sum(oriented * oriented)  2.19 us

profile of v2, /device:TPU:0, one launch (start us, length us, event | category | flops | bytes accessed | tf_op | source)
XLA Modules:
  0.0 83.9 jit_solution(1258088517197136)
XLA Ops:
  0.6 31.5 %shard_map.58 = (f32[512,512]{1,0:T(8,128)}, f32[512,512]{1,0:T(8,128)}) custom-call(s32[4]{0:T(128)} %owners.3, bf16[128,1024]{1,0:T(8,128)(2,1)} %acts.1, bf16[128,1024]{1,0:T(8,128)(2,1)} %cots.1), custom_call_target="tpu_custom_call" | custom-call | tf_op jit(solution)/shard_map/pallas_call | solution.py:256
  32.1 2.2 %multiply_reduce_fusion.1 = f32[]{:T(128)} fusion(f32[512,512]{1,0:T(8,128)} %get-tuple-element.7), kind=kLoop, calls=%fused_computation.17 | loop fusion | flops 524287 | bytes 1048580 | tf_op jit(solution)/shard_map/reduce_sum | solution.py:272
  35.0 1.8 %multiply_reduce_fusion = (f32[]{:T(128)}, f32[512,512]{1,0:T(8,128)S(1)}) fusion(f32[]{:T(128)S(6)} %mul_shard_map.7, f32[512,512]{1,0:T(8,128)S(1)} %copy-done.1), kind=kOutput, calls=%fused_computation.15 | convolution fusion | flops 806617088 | bytes 2097160 | tf_op jit(solution)/shard_map/dot_general | solution.py:228
  37.5 1.0 %fusion.34 = f32[512,512]{1,0:T(8,128)S(1)} fusion(f32[512,512]{1,0:T(8,128)S(1)} %get-tuple-element.12, f32[]{:T(128)S(6)} %sqrt.3), kind=kOutput, calls=%fused_computation.46 | convolution fusion | flops 805568512 | bytes 2097156 | tf_op jit(solution)/shard_map/dot_general | solution.py:228
  38.5 1.2 %fusion.6 = f32[512,512]{1,0:T(8,128)S(1)} fusion(f32[512,512]{1,0:T(8,128)S(1)} %fusion.34, f32[512,512]{1,0:T(8,128)S(1)} %get-tuple-element.12, f32[]{:T(128)S(6)} %sqrt.3), kind=kOutput, calls=%fused_computation.9 | convolution fusion | flops 807141376 | bytes 3145732 | tf_op jit(solution)/shard_map/dot_general | solution.py:228
  39.7 0.0 copy-done.4
  39.7 1.1 %convolution_subtract_fusion.1 = f32[512,512]{1,0:T(8,128)S(1)} fusion(f32[512,512]{1,0:T(8,128)S(1)} %fusion.6, f32[512,512]{1,0:T(8,128)S(1)} %fusion.34, f32[512,512]{1,0:T(8,128)S(1)} %get-tuple-element.12, f32[]{:T(128)S(6)} %sqrt.3), kind=kOutput, calls=%fused_computation.2 | convolution fusion | flops 807927808 | bytes 4194308 | tf_op jit(solution)/shard_map/dot_general | solution.py:228
  40.8 1.0 %fusion.14 = f32[512,512]{1,0:T(8,128)S(1)} fusion(f32[512,512]{1,0:T(8,128)S(1)} %convolution_subtract_fusion.1), kind=kOutput, calls=%fused_computation.20 | convolution fusion | flops 805568512 | bytes 2097152 | tf_op jit(solution)/shard_map/dot_general | solution.py:228
  41.9 0.0 copy-start.5
  41.9 1.0 %fusion.35 = f32[512,512]{1,0:T(8,128)S(1)} fusion(f32[512,512]{1,0:T(8,128)S(1)} %fusion.14), kind=kOutput, calls=%fused_computation.47 | convolution fusion | flops 805306368 | bytes 2097152 | tf_op jit(solution)/shard_map/dot_general | solution.py:228
  42.9 0.2 copy-done.5
  43.1 2.0 %fusion.12 = f32[512,512]{1,0:T(8,128)} fusion(f32[512,512]{1,0:T(8,128)S(1)} %convolution_subtract_fusion.1, f32[512,512]{1,0:T(8,128)S(1)} %copy-done.5, f32[]{:T(128)S(6)} %sqrt.3), kind=kOutput, calls=%fused_computation.18 | convolution fusion | flops 805830656 | bytes 3145732 | tf_op jit(solution)/shard_map/dot_general | solution.py:228
  45.2 2.6 %fusion = f32[512,512]{1,0:T(8,128)S(1)} fusion(f32[512,512]{1,0:T(8,128)S(1)} %fusion.35, f32[512,512]{1,0:T(8,128)} %fusion.12, f32[512,512]{1,0:T(8,128)} %copy-done.3, f32[]{:T(128)S(6)} %mul.80), kind=kOutput, calls=%fused_computation.1 | convolution fusion | flops 806092800 | bytes 4194308 | tf_op jit(solution)/shard_map/dot_general | solution.py:228
  47.8 0.0 copy-start
  47.9 0.0 copy-start.6
  47.9 0.7 copy-done.6
  48.6 0.6 compare_reduce_fusion
  49.2 0.9 %fusion.16 = f32[2,1,128,512]{3,2,1,0:T(8,128)S(1)} fusion(f32[2,2,128,512]{3,2,1,0:T(8,128)S(1)} %bitcast.16, f32[2,2,128,512]{3,2,1,0:T(8,128)S(1)} %bitcast.15, pred[]{:T(512)S(6)} %eq.32, pred[]{:T(512)} %compare_reduce_fusion), kind=kLoop, calls=%fused_computation.23 | loop fusion | flops 393216 | bytes 2621442 | tf_op jit(solution)/shard_map/jit(_where)/select_n | solution.py:283
  50.1 0.6 fusion.36
  50.7 2.7 %multiply_reduce_fusion.2 = (f32[]{:T(128)}, f32[256,512]{1,0:T(8,128)}) fusion(f32[256,512]{1,0:T(8,128)S(1)} %fusion.36, f32[512,512]{1,0:T(8,128)S(1)} %copy-done.2, f32[512,512]{1,0:T(8,128)S(1)} %fusion, pred[]{:T(512)} %compare_reduce_fusion), kind=kOutput, calls=%fused_computation.25 | convolution fusion | flops 403177472 | bytes 3145733 | tf_op jit(solution)/shard_map/dot_general | solution.py:228
  54.1 0.7 compare_select_fusion
  54.8 0.7 iota.31.stats
  55.5 25.1 %shard_map.59 = (bf16[128,1024]{1,0:T(8,128)(2,1)}, f32[1,1]{1,0:T(1,128)}) custom-call(s32[4]{0:T(128)} %owners.3, f32[8,128]{1,0:T(8,128)} %iota.31.stats, f32[2,128,512]{2,1,0:T(8,128)} %bitcast.18), custom_call_target="tpu_custom_call" | custom-call | tf_op jit(solution)/shard_map/pallas_call | solution.py:288
  80.5 1.7 %copy.8 = bf16[128,1024]{1,0:T(8,128)(2,1)} copy(bf16[128,1024]{1,0:T(8,128)(2,1)} %get-tuple-element.18) | data formatting | bytes 524288
  (8 shorter events, 0.0 us)
Async XLA Ops:
  32.1 2.9 %copy-start.1 = (f32[512,512]{1,0:T(8,128)S(1)}, f32[512,512]{1,0:T(8,128)}, u32[]{:S(2)}) copy-start(f32[512,512]{1,0:T(8,128)} %get-tuple-element.7) | copy-start | bytes 3145732
  36.8 3.0 %copy-start.4 = (f32[512,512]{1,0:T(8,128)}, f32[512,512]{1,0:T(8,128)S(1)}, u32[]{:S(2)}) copy-start(f32[512,512]{1,0:T(8,128)S(1)} %get-tuple-element.12) | copy-start | bytes 3145732
  40.8 2.1 %copy-start.3 = (f32[512,512]{1,0:T(8,128)}, f32[512,512]{1,0:T(8,128)S(1)}, u32[]{:S(2)}) copy-start(f32[512,512]{1,0:T(8,128)S(1)} %convolution_subtract_fusion.1) | copy-start | bytes 3145732
  41.9 1.2 %copy-start.5 = (f32[512,512]{1,0:T(8,128)S(1)}, f32[512,512]{1,0:T(8,128)}, u32[]{:S(2)}) copy-start(f32[512,512]{1,0:T(8,128)} %copy-done.4) | copy-start | bytes 3145732
  45.2 4.0 %copy-start.2 = (f32[512,512]{1,0:T(8,128)S(1)}, f32[512,512]{1,0:T(8,128)}, u32[]{:S(2)}) copy-start(f32[512,512]{1,0:T(8,128)} %get-tuple-element.8) | copy-start | bytes 3145732
  47.8 2.9 %copy-start = (f32[512,512]{1,0:T(8,128)}, f32[512,512]{1,0:T(8,128)S(1)}, u32[]{:S(2)}) copy-start(f32[512,512]{1,0:T(8,128)S(1)} %fusion) | copy-start | bytes 3145732
  47.9 0.7 copy-start.6

commit v3 on v2

--- a/solution.py
+++ b/solution.py
@@ -13,7 +13,44 @@
 MESH = pl.DeviceIdType.MESH
 
 
-def gather_kernel(dp, mp, owners, acts, cots, grad, oriented, a_sel, c_sel, a_all, c_all, az_send, ax_send, am_send, cz_send, cx_send, a_recv, c_recv):
+def split(x):
+    high = x.astype(jnp.bfloat16)
+    return high, (x - high.astype(jnp.float32)).astype(jnp.bfloat16)
+
+
+def product(left, right, transposed=False):
+    a, b = split(left), split(right)
+    axis = 1 if transposed else 0
+    return lax.dot_general(
+        jnp.concatenate([a[0], a[0], a[1]], axis=1),
+        jnp.concatenate([b[0], b[1], b[0]], axis=axis),
+        (((1,), (axis,)), ((), ())),
+        preferred_element_type=jnp.float32,
+    )
+
+
+def total(x):
+    return jnp.sum(jnp.sum(x, axis=0, keepdims=True), axis=1, keepdims=True)
+
+
+def inverse_root(stat, eye):
+    size = jnp.sqrt(total(stat * stat))
+    m = stat / size
+    m2 = product(m, m)
+    f = (5.0 * eye - m) * 0.25
+    f2 = (25.0 * eye - 10.0 * m + m2) * 0.0625
+    mf = (5.0 * m - m2) * 0.25
+    y = (5.0 * f - product(product(f2, f2), mf)) * 0.25
+    my = product(m, y)
+    y2 = product(y, y)
+    return (5.0 * y - product(product(y2, y2), my)) * (0.25 / jnp.sqrt(jnp.sqrt(size)))
+
+
+def step_kernel(
+    dp, mp, owners, acts, cots, update, root, graft_ref, grad, oriented, a_sel, c_sel, a_all, c_all,
+    stats, slots, pre, out, got,
+    az_send, ax_send, am_send, cz_send, cx_send, a_recv, c_recv, m_send, m_recv, d_send, d_recv, u_send, u_recv,
+):
     pairs = dp // 2
     me = lax.axis_index("dp")
     col = lax.axis_index("mp")
@@ -25,9 +62,8 @@
         return 2 * lax.rem(pair + k, pairs) + side
 
     barrier = pltpu.get_barrier_semaphore()
-    for k in range(1, pairs):
-        pl.semaphore_signal(barrier, inc=1, device_id=(source(k), col), device_id_type=MESH)
-    pl.semaphore_signal(barrier, inc=1, device_id=(across, col), device_id_type=MESH)
+    for k in range(1, dp):
+        pl.semaphore_signal(barrier, inc=1, device_id=(lax.rem(me + k, dp), col), device_id_type=MESH)
     for k in range(1, mp):
         pl.semaphore_signal(barrier, inc=1, device_id=(me, lax.rem(col + k, mp)), device_id_type=MESH)
 
@@ -54,7 +90,7 @@
         jnp.add, [jnp.where(owners[b] == me, 1.0, 0.0) for b in range(owners.shape[0])])
     a_all[me, col] = a_sel[pair]
     c_all[me] = c_sel[pair]
-    pl.semaphore_wait(barrier, pairs - 1 + 1 + mp - 1)
+    pl.semaphore_wait(barrier, dp - 1 + mp - 1)
 
     def a_pair(k):
         dest = lax.rem(pair + k, pairs)
@@ -147,35 +183,23 @@
         accumulate(k - 1)
     accumulate(pairs - 1)
 
-    @pl.loop(0, dp)
-    def _(src):
-        @pl.loop(1, mp)
-        def _(k):
-            a_mp(src, k).wait_send()
-
-    for k in range(pairs):
-        a_across(k).wait_send()
-        c_across(k).wait_send()
-    for k in order:
-        a_pair(k).wait_send()
-        c_pair(k).wait_send()
-
-
-def finish_kernel(dp, mp, owners, stats, pre, update, graft_ref, slots, out, got, m_send, m_recv, d_send, d_recv, u_send, u_recv):
-    pairs = dp // 2
-    halves = pre.shape[0]
-    me = lax.axis_index("dp")
-    col = lax.axis_index("mp")
-    pair = me // 2
-    side = me % 2
-
-    barrier = pltpu.get_barrier_semaphore()
-    for k in range(1, dp):
-        pl.semaphore_signal(barrier, inc=1, device_id=(lax.rem(me + k, dp), col), device_id_type=MESH)
-    for k in range(1, mp):
-        pl.semaphore_signal(barrier, inc=1, device_id=(me, lax.rem(col + k, mp)), device_id_type=MESH)
+    g = oriented[...]
+    grad_total = total(g * g)
+    ids = lax.broadcasted_iota(jnp.int32, (B, B), 0), lax.broadcasted_iota(jnp.int32, (B, B), 1)
+    eye = jnp.where(ids[0] == ids[1], 1.0, 0.0)
+    ridge = 0.1 * (grad_total / B + 1.0)
+    root[...] = inverse_root(product(g, g, transposed=True) + ridge * eye, eye)
+    is_right = 1.0 - is_left
+    halves, rows = out.shape[:2]
+    starts = [pl.multiple_of((2 * h + side) * rows, rows) for h in range(halves)]
+    first = jnp.concatenate(
+        [root[pl.ds(n, rows), :] * is_left + grad[pl.ds(n, rows), :] * is_right for n in starts], axis=0)
+    last = grad[...] * is_left + root[...] * is_right
+    mine = product(product(first, root[...]), last)
+    row_ids = lax.broadcasted_iota(jnp.int32, stats.shape, 0)
+    stats[...] = jnp.where(row_ids == 0, 0.5 * grad_total, total(mine * mine))
     slots[me, col] = stats[...]
-    pl.semaphore_wait(barrier, dp - 1 + mp - 1)
+    pre[...] = mine.reshape(halves, rows, B)
 
     def over_mp(k):
         return pltpu.make_async_remote_copy(
@@ -216,6 +240,18 @@
     for c in range(CB):
         holder = owners[(pair // halves) * CB + c] // 2
         update[:, c * B : (c + 1) * B] = got[holder]
+    @pl.loop(0, dp)
+    def _(src):
+        @pl.loop(1, mp)
+        def _(k):
+            a_mp(src, k).wait_send()
+
+    for k in range(pairs):
+        a_across(k).wait_send()
+        c_across(k).wait_send()
+    for k in order:
+        a_pair(k).wait_send()
+        c_pair(k).wait_send()
     for k in range(1, mp):
         over_mp(k).wait_send()
     for k in range(1, dp):
@@ -224,83 +260,43 @@
         piece(k).wait_send()
 
 
-def product(left, right):
-    return jnp.matmul(left, right, precision=lax.Precision.HIGH, preferred_element_type=jnp.float32)
-
-
-def inverse_root(stat):
-    eye = jnp.eye(B, dtype=jnp.float32)
-    size = jnp.sqrt(jnp.sum(stat * stat))
-    m = stat / size
-    m2 = product(m, m)
-    f = (5.0 * eye - m) * 0.25
-    f2 = (25.0 * eye - 10.0 * m + m2) * 0.0625
-    mf = (5.0 * m - m2) * 0.25
-    y = (5.0 * f - product(product(f2, f2), mf)) * 0.25
-    my = product(m, y)
-    y2 = product(y, y)
-    return (5.0 * y - product(product(y2, y2), my)) * (0.25 * size ** (-0.25))
-
-
 def on_device(activations, cotangents, owners):
     dp = lax.axis_size("dp")
     mp = lax.axis_size("mp")
-    me = lax.axis_index("dp")
     pairs = dp // 2
     tokens, features = activations.shape
     part = tokens // mp
+    rows = features // dp
+    halves = B // rows // 2
     vmem = pl.BlockSpec(memory_space=pltpu.VMEM)
     smem = pl.BlockSpec(memory_space=pltpu.SMEM)
     dma = pltpu.SemaphoreType.DMA
-    square = jax.ShapeDtypeStruct((B, B), jnp.float32)
-    gradient, oriented = pl.pallas_call(
-        functools.partial(gather_kernel, dp, mp),
-        out_shape=(square, square),
+    update, root, graft = pl.pallas_call(
+        functools.partial(step_kernel, dp, mp),
+        out_shape=(
+            jax.ShapeDtypeStruct((rows, CB * B), jnp.bfloat16),
+            jax.ShapeDtypeStruct((B, B), jnp.float32),
+            jax.ShapeDtypeStruct((1, 1), jnp.float32),
+        ),
         in_specs=[smem, vmem, vmem],
-        out_specs=(vmem, vmem),
+        out_specs=(vmem, vmem, smem),
         scratch_shapes=[
+            pltpu.VMEM((B, B), jnp.float32),
+            pltpu.VMEM((B, B), jnp.float32),
             pltpu.VMEM((pairs, part, B), jnp.bfloat16),
             pltpu.VMEM((pairs, tokens, B), jnp.bfloat16),
             pltpu.VMEM((dp, mp, part, B), jnp.bfloat16),
             pltpu.VMEM((dp, tokens, B), jnp.bfloat16),
+            pltpu.VMEM((8, 128), jnp.float32),
+            pltpu.VMEM((dp, mp, 8, 128), jnp.float32),
+            pltpu.VMEM((halves, rows, B), jnp.float32),
+            pltpu.VMEM((halves, rows, B), jnp.bfloat16),
+            pltpu.VMEM((pairs, rows, B), jnp.bfloat16),
             dma((pairs,)), dma((pairs,)), dma((dp, mp)), dma((pairs,)), dma((pairs,)), dma((dp, mp)), dma((dp,)),
+            dma((mp,)), dma((mp,)), dma((dp,)), dma((dp,)), dma((pairs,)), dma((pairs,)),
         ],
         compiler_params=pltpu.CompilerParams(collective_id=0, has_side_effects=True),
     )(owners, activations, cotangents)
-
-    my_left = jnp.any(owners == me)
-    grad_total = jnp.sum(oriented * oriented)
-    ridge = 0.1 * (grad_total / B + 1.0) * jnp.eye(B, dtype=jnp.float32)
-    root = inverse_root(product(oriented, oriented.T) + ridge)
-
-    rows = features // dp
-    halves = B // rows // 2
-
-    def my_rows(matrix):
-        split = matrix.reshape(halves, 2, rows, B)
-        return jnp.where(me % 2 == 0, split[:, 0], split[:, 1]).reshape(halves * rows, B)
-
-    first = jnp.where(my_left, my_rows(root), my_rows(gradient))
-    last = jnp.where(my_left, gradient, root)
-    pre = product(product(first, root), last)
-    row_ids = lax.broadcasted_iota(jnp.int32, (8, 128), 0)
-    stats = jnp.where(row_ids == 0, 0.5 * grad_total, jnp.sum(pre * pre))
-    update, graft = pl.pallas_call(
-        functools.partial(finish_kernel, dp, mp),
-        out_shape=(
-            jax.ShapeDtypeStruct((rows, CB * B), jnp.bfloat16),
-            jax.ShapeDtypeStruct((1, 1), jnp.float32),
-        ),
-        in_specs=[smem, vmem, vmem],
-        out_specs=(vmem, smem),
-        scratch_shapes=[
-            pltpu.VMEM((dp, mp, 8, 128), jnp.float32),
-            pltpu.VMEM((halves, rows, B), jnp.bfloat16),
-            pltpu.VMEM((pairs, rows, B), jnp.bfloat16),
-            dma((mp,)), dma((mp,)), dma((dp,)), dma((dp,)), dma((pairs,)), dma((pairs,)),
-        ],
-        compiler_params=pltpu.CompilerParams(collective_id=1, has_side_effects=True),
-    )(owners, stats, pre.reshape(halves, rows, B))
     return (update, root, graft[0, 0])
 
 

time: 84.3 us -> 67.6 us (0.80)
  matrix products: 15.1 us -> 0 us
  Pallas kernels: 56.6 us -> 61 us
  other arithmetic: 4.37 us -> 0 us
  between operations: 4.63 us -> 2.39 us
    dot_general x10 -> x0, matrix products: 15.1 us -> none  [product(): jnp.matmul(left, right, precision=lax.Precision.HIGH, preferred_element_t...]
    pallas_call x2 -> x1, Pallas kernels: 56.6 us -> 61 us  [on_device(): pl.pallas_call(functools.partial(step_kernel, dp, mp), out_shape=(jax.Sha...]
    reduce_sum x1 -> x0, other arithmetic: 2.19 us -> none  [on_device(): grad_total = jnp.sum(oriented * oriented)]
    select_n x2 -> x0, other arithmetic: 1.56 us -> none  [the longest x1 0.86 us: on_device(): first = jnp.where(my_left, my_rows(root), my_rows(gradient))]
    unnamed x15 -> x2, local copies, waits for them, and re-layouts: 2.58 us -> 3.93 us
where the time goes in v3:
time: 67.6 us; the launch traced here: 67.4 us
  Pallas kernels  61 us (90%)
  local copies, waits for them, and re-layouts  3.93 us (6%)
  between operations  2.39 us (4%)
    pallas_call x1, Pallas kernels, on_device(): pl.pallas_call(functools.partial(step_kernel, dp, mp), out_shape=(jax.Sha...  61 us
    unnamed x2, local copies, waits for them, and re-layouts  3.93 us

profile of v3, /device:TPU:0, one launch (start us, length us, event | category | flops | bytes accessed | tf_op | source)
XLA Modules:
  0.0 67.4 jit_solution(14637155855124004585)
XLA Ops:
  0.6 61.0 %shard_map.58 = (bf16[128,1024]{1,0:T(8,128)(2,1)}, f32[512,512]{1,0:T(8,128)}, f32[1,1]{1,0:T(1,128)}) custom-call(s32[4]{0:T(128)} %owners.1, bf16[128,1024]{1,0:T(8,128)(2,1)} %acts.1, bf16[128,1024]{1,0:T(8,128)(2,1)} %cots.1), custom_call_target="tpu_custom_call" | custom-call | tf_op jit(solution)/shard_map/pallas_call | solution.py:274
  61.7 1.7 %copy.9 = bf16[128,1024]{1,0:T(8,128)(2,1)} copy(bf16[128,1024]{1,0:T(8,128)(2,1)} %get-tuple-element.12) | data formatting | bytes 524288
  63.3 2.3 %copy.10 = f32[512,512]{1,0:T(8,128)} copy(f32[512,512]{1,0:T(8,128)} %get-tuple-element.13) | data formatting | bytes 2097152

commit v4 on v3

--- a/solution.py
+++ b/solution.py
@@ -10,6 +10,7 @@
 
 B = 512
 CB = 2
+CHUNKS = 2
 MESH = pl.DeviceIdType.MESH
 
 
@@ -43,11 +44,11 @@
     y = (5.0 * f - product(product(f2, f2), mf)) * 0.25
     my = product(m, y)
     y2 = product(y, y)
-    return (5.0 * y - product(product(y2, y2), my)) * (0.25 / jnp.sqrt(jnp.sqrt(size)))
+    return (5.0 * y - product(product(y2, y2), my)) * 0.25, 1.0 / jnp.sqrt(jnp.sqrt(size))
 
 
 def step_kernel(
-    dp, mp, owners, acts, cots, update, root, graft_ref, grad, oriented, a_sel, c_sel, a_all, c_all,
+    dp, mp, owners, acts_in, cots_in, update, root, scale_ref, graft_ref, acts, cots, in_sem, grad, oriented, a_sel, c_sel, a_all, c_all,
     stats, slots, pre, out, got,
     az_send, ax_send, am_send, cz_send, cx_send, a_recv, c_recv, m_send, m_recv, d_send, d_recv, u_send, u_recv,
 ):
@@ -66,6 +67,15 @@
         pl.semaphore_signal(barrier, inc=1, device_id=(lax.rem(me + k, dp), col), device_id_type=MESH)
     for k in range(1, mp):
         pl.semaphore_signal(barrier, inc=1, device_id=(me, lax.rem(col + k, mp)), device_id_type=MESH)
+
+    fetches = [
+        pltpu.make_async_copy(acts_in, acts, in_sem.at[0]),
+        pltpu.make_async_copy(cots_in, cots, in_sem.at[1]),
+    ]
+    for fetch in fetches:
+        fetch.start()
+    for fetch in fetches:
+        fetch.wait()
 
     def block_of(which):
         held = [jnp.where(owners[b] // 2 == which, b, 0) for b in range(owners.shape[0])]
@@ -97,10 +107,13 @@
         return pltpu.make_async_remote_copy(
             a_sel.at[dest], a_all.at[me, col], az_send.at[k], a_recv.at[me, col], (source(k), col), MESH)
 
-    def c_pair(k):
+    chunk = cots.shape[0] // CHUNKS
+
+    def c_pair(k, h):
         dest = lax.rem(pair + k, pairs)
-        return pltpu.make_async_remote_copy(
-            c_sel.at[dest], c_all.at[me], cz_send.at[k], c_recv.at[me], (source(k), col), MESH)
+        cut = pl.ds(h * chunk, chunk)
+        return pltpu.make_async_remote_copy(
+            c_sel.at[dest, cut], c_all.at[me, cut], cz_send.at[k, h], c_recv.at[me, h], (source(k), col), MESH)
 
     def a_across(k):
         src = source(k)
@@ -108,11 +121,12 @@
         return pltpu.make_async_remote_copy(
             ref, a_all.at[src, col], ax_send.at[k], a_recv.at[src, col], (across, col), MESH)
 
-    def c_across(k):
+    def c_across(k, h):
         src = source(k)
-        ref = c_sel.at[pair] if k == 0 else c_all.at[src]
-        return pltpu.make_async_remote_copy(
-            ref, c_all.at[src], cx_send.at[k], c_recv.at[src], (across, col), MESH)
+        cut = pl.ds(h * chunk, chunk)
+        ref = c_sel.at[pair, cut] if k == 0 else c_all.at[src, cut]
+        return pltpu.make_async_remote_copy(
+            ref, c_all.at[src, cut], cx_send.at[k, h], c_recv.at[src, h], (across, col), MESH)
 
     def a_mp(src, k, own=False):
         ref = a_sel.at[pair] if own else a_all.at[src, col]
@@ -127,16 +141,18 @@
     def a_arrived(src, who):
         pltpu.make_async_copy(a_all.at[src, who], a_all.at[src, who], a_recv.at[src, who]).wait()
 
-    def c_arrived(src):
-        pltpu.make_async_copy(c_all.at[src], c_all.at[src], c_recv.at[src]).wait()
+    def c_arrived(src, h):
+        ref = c_all.at[src, pl.ds(h * chunk, chunk)]
+        pltpu.make_async_copy(ref, ref, c_recv.at[src, h]).wait()
 
     order = list(range(1, pairs))
     a_across(0).start()
     for k in order:
         a_pair(k).start()
-    c_across(0).start()
-    for k in order:
-        c_pair(k).start()
+    for h in range(CHUNKS):
+        c_across(0, h).start()
+        for k in order:
+            c_pair(k, h).start()
 
     @pl.loop(1, mp)
     def _(k):
@@ -159,7 +175,8 @@
         base = 2 * lax.rem(pair + k, pairs)
         a_complete(base)
         a_complete(base + 1)
-        c_arrived(source(k) + 1 - 2 * side)
+        for h in range(CHUNKS):
+            c_arrived(source(k) + 1 - 2 * side, h)
         tokens = 2 * cots.shape[0]
         a = a_all[pl.ds(base, 2)].reshape(tokens, B)
         c = c_all[pl.ds(base, 2)].reshape(tokens, B)
@@ -177,10 +194,12 @@
             grad[...] += add
             oriented[...] += add_oriented
 
-    for k in order:
-        c_arrived(source(k))
-        c_across(k).start()
-        accumulate(k - 1)
+    for h in range(CHUNKS):
+        for k in order:
+            c_arrived(source(k), h)
+            c_across(k, h).start()
+            if h == CHUNKS - 1:
+                accumulate(k - 1)
     accumulate(pairs - 1)
 
     g = oriented[...]
@@ -188,14 +207,15 @@
     ids = lax.broadcasted_iota(jnp.int32, (B, B), 0), lax.broadcasted_iota(jnp.int32, (B, B), 1)
     eye = jnp.where(ids[0] == ids[1], 1.0, 0.0)
     ridge = 0.1 * (grad_total / B + 1.0)
-    root[...] = inverse_root(product(g, g, transposed=True) + ridge * eye, eye)
+    root[...], factor = inverse_root(product(g, g, transposed=True) + ridge * eye, eye)
+    scale_ref[0, 0] = factor[0, 0]
     is_right = 1.0 - is_left
     halves, rows = out.shape[:2]
     starts = [pl.multiple_of((2 * h + side) * rows, rows) for h in range(halves)]
     first = jnp.concatenate(
         [root[pl.ds(n, rows), :] * is_left + grad[pl.ds(n, rows), :] * is_right for n in starts], axis=0)
     last = grad[...] * is_left + root[...] * is_right
-    mine = product(product(first, root[...]), last)
+    mine = product(product(first, root[...]), last) * (factor * factor)
     row_ids = lax.broadcasted_iota(jnp.int32, stats.shape, 0)
     stats[...] = jnp.where(row_ids == 0, 0.5 * grad_total, total(mine * mine))
     slots[me, col] = stats[...]
@@ -239,7 +259,7 @@
         pltpu.make_async_copy(got.at[who], got.at[who], u_recv.at[who]).wait()
     for c in range(CB):
         holder = owners[(pair // halves) * CB + c] // 2
-        update[:, c * B : (c + 1) * B] = got[holder]
+        update[c] = got[holder]
     @pl.loop(0, dp)
     def _(src):
         @pl.loop(1, mp)
@@ -248,10 +268,12 @@
 
     for k in range(pairs):
         a_across(k).wait_send()
-        c_across(k).wait_send()
+        for h in range(CHUNKS):
+            c_across(k, h).wait_send()
     for k in order:
         a_pair(k).wait_send()
-        c_pair(k).wait_send()
+        for h in range(CHUNKS):
+            c_pair(k, h).wait_send()
     for k in range(1, mp):
         over_mp(k).wait_send()
     for k in range(1, dp):
@@ -270,17 +292,22 @@
     halves = B // rows // 2
     vmem = pl.BlockSpec(memory_space=pltpu.VMEM)
     smem = pl.BlockSpec(memory_space=pltpu.SMEM)
+    anywhere = pl.BlockSpec(memory_space=pl.ANY)
     dma = pltpu.SemaphoreType.DMA
-    update, root, graft = pl.pallas_call(
+    update, root, scale, graft = pl.pallas_call(
         functools.partial(step_kernel, dp, mp),
         out_shape=(
-            jax.ShapeDtypeStruct((rows, CB * B), jnp.bfloat16),
+            jax.ShapeDtypeStruct((CB, rows, B), jnp.bfloat16),
             jax.ShapeDtypeStruct((B, B), jnp.float32),
             jax.ShapeDtypeStruct((1, 1), jnp.float32),
+            jax.ShapeDtypeStruct((1, 1), jnp.float32),
         ),
-        in_specs=[smem, vmem, vmem],
-        out_specs=(vmem, vmem, smem),
+        in_specs=[smem, anywhere, anywhere],
+        out_specs=(vmem, vmem, smem, smem),
         scratch_shapes=[
+            pltpu.VMEM(activations.shape, jnp.bfloat16),
+            pltpu.VMEM(cotangents.shape, jnp.bfloat16),
+            dma((2,)),
             pltpu.VMEM((B, B), jnp.float32),
             pltpu.VMEM((B, B), jnp.float32),
             pltpu.VMEM((pairs, part, B), jnp.bfloat16),
@@ -292,12 +319,12 @@
             pltpu.VMEM((halves, rows, B), jnp.float32),
             pltpu.VMEM((halves, rows, B), jnp.bfloat16),
             pltpu.VMEM((pairs, rows, B), jnp.bfloat16),
-            dma((pairs,)), dma((pairs,)), dma((dp, mp)), dma((pairs,)), dma((pairs,)), dma((dp, mp)), dma((dp,)),
+            dma((pairs,)), dma((pairs,)), dma((dp, mp)), dma((pairs, CHUNKS)), dma((pairs, CHUNKS)), dma((dp, mp)), dma((dp, CHUNKS)),
             dma((mp,)), dma((mp,)), dma((dp,)), dma((dp,)), dma((pairs,)), dma((pairs,)),
         ],
         compiler_params=pltpu.CompilerParams(collective_id=0, has_side_effects=True),
     )(owners, activations, cotangents)
-    return (update, root, graft[0, 0])
+    return (jnp.concatenate([update[c] for c in range(CB)], axis=1), root * scale, graft[0, 0])
 
 
 def solution(mesh):

time: 67.6 us -> 66.1 us (0.978)
  local copies, waits for them, and re-layouts: 3.93 us -> 1.08 us
  other arithmetic: 0 us -> 2.36 us
  Pallas kernels: 61 us -> 60.1 us
    unnamed x2, local copies, waits for them, and re-layouts: 3.93 us -> 0.01 us
    mul x0 -> x1, other arithmetic: none -> 1.63 us  [on_device(): root * scale]
    squeeze x0 -> x1, local copies, waits for them, and re-layouts: none -> 1.07 us  [on_device(): update[c]]
    pallas_call x1, Pallas kernels: 61 us -> 60.1 us  [on_device(): pl.pallas_call(functools.partial(step_kernel, dp, mp), out_shape=(jax.Sha...]
    concatenate x0 -> x1, other arithmetic: none -> 0.73 us  [on_device(): jnp.concatenate([update[c] for c in range(CB)], axis=1)]
where the time goes in v4:
time: 66.1 us; the launch traced here: 65.9 us
  Pallas kernels  60.1 us (91%)
  between operations  2.41 us (4%)
  other arithmetic  2.36 us (4%)
  local copies, waits for them, and re-layouts  1.08 us (2%)
    pallas_call x1, Pallas kernels, on_device(): pl.pallas_call(functools.partial(step_kernel, dp, mp), out_shape=(jax.Sha...  60.1 us
    mul x1, other arithmetic, on_device(): root * scale  1.63 us

profile of v4, /device:TPU:0, one launch (start us, length us, event | category | flops | bytes accessed | tf_op | source)
XLA Modules:
  0.0 65.9 jit_solution(6643886143907502302)
XLA Ops:
  0.6 60.1 %shard_map.58 = (bf16[2,128,512]{2,1,0:T(8,128)(2,1)}, f32[512,512]{1,0:T(8,128)}, f32[1,1]{1,0:T(1,128)}, f32[1,1]{1,0:T(1,128)}) custom-call(s32[4]{0:T(128)} %owners.1, bf16[128,1024]{1,0:T(8,128)(2,1)} %acts_in.1, bf16[128,1024]{1,0:T(8,128)(2,1)} %cots_in.1), custom_call_target="tpu_custom_call" | custom-call | tf_op jit(solution)/shard_map/pallas_call | solution.py:297
  60.7 0.0 copy-start
  60.7 1.1 %slice_bitcast_fusion.1 = (bf16[128,512]{1,0:T(8,128)(2,1)S(1)}, bf16[128,512]{1,0:T(8,128)(2,1)S(1)}) fusion(bf16[2,128,512]{2,1,0:T(8,128)(2,1)} %get-tuple-element.7), kind=kLoop, calls=%fused_computation.3 | loop fusion | bytes 524288 | tf_op jit(solution)/shard_map/squeeze | solution.py:327
  61.8 0.7 %pad_maximum_fusion = bf16[128,1024]{1,0:T(8,128)(2,1)} fusion(bf16[128,512]{1,0:T(8,128)(2,1)S(1)} %get-tuple-element.12, bf16[128,512]{1,0:T(8,128)(2,1)S(1)} %get-tuple-element.11), kind=kLoop, calls=%fused_computation.1 | loop fusion | flops 524288 | bytes 524288 | tf_op jit(solution)/shard_map/concatenate | solution.py:327
  62.5 0.0 copy-done
  62.5 1.6 %broadcast_multiply_fusion = f32[512,512]{1,0:T(8,128)} fusion(f32[512,512]{1,0:T(8,128)S(1)} %copy-done, f32[]{:T(128)} %bitcast.2), kind=kLoop, calls=%fused_computation | loop fusion | flops 262144 | bytes 2097156 | tf_op jit(solution)/shard_map/mul | solution.py:327
Async XLA Ops:
  60.7 1.8 %copy-start = (f32[512,512]{1,0:T(8,128)S(1)}, f32[512,512]{1,0:T(8,128)}, u32[]{:S(2)}) copy-start(f32[512,512]{1,0:T(8,128)} %get-tuple-element.8) | copy-start | bytes 3145732

commit v5 on v4

--- a/solution.py
+++ b/solution.py
@@ -48,9 +48,9 @@
 
 
 def step_kernel(
-    dp, mp, owners, acts_in, cots_in, update, root, scale_ref, graft_ref, acts, cots, in_sem, grad, oriented, a_sel, c_sel, a_all, c_all,
+    dp, mp, owners, acts, cots, update, root, scale_ref, graft_ref, grad, oriented, a_sel, c_sel, a_all, c_all,
     stats, slots, pre, out, got,
-    az_send, ax_send, am_send, cz_send, cx_send, a_recv, c_recv, m_send, m_recv, d_send, d_recv, u_send, u_recv,
+    az_send, ax_send, am_send, cz_send, cx_send, a_recv, c_recv, d_send, d_recv, u_send, u_recv,
 ):
     pairs = dp // 2
     me = lax.axis_index("dp")
@@ -63,19 +63,17 @@
         return 2 * lax.rem(pair + k, pairs) + side
 
     barrier = pltpu.get_barrier_semaphore()
-    for k in range(1, dp):
-        pl.semaphore_signal(barrier, inc=1, device_id=(lax.rem(me + k, dp), col), device_id_type=MESH)
-    for k in range(1, mp):
-        pl.semaphore_signal(barrier, inc=1, device_id=(me, lax.rem(col + k, mp)), device_id_type=MESH)
-
-    fetches = [
-        pltpu.make_async_copy(acts_in, acts, in_sem.at[0]),
-        pltpu.make_async_copy(cots_in, cots, in_sem.at[1]),
-    ]
-    for fetch in fetches:
-        fetch.start()
-    for fetch in fetches:
-        fetch.wait()
+    count = dp * mp
+    flat = me * mp + col
+
+    def peer(k):
+        other = lax.rem(flat + k, count)
+        return other // mp, lax.rem(other, mp)
+
+    @pl.loop(1, count)
+    def _(k):
+        pl.semaphore_signal(barrier, inc=1, device_id=peer(k), device_id_type=MESH)
+
 
     def block_of(which):
         held = [jnp.where(owners[b] // 2 == which, b, 0) for b in range(owners.shape[0])]
@@ -100,7 +98,7 @@
         jnp.add, [jnp.where(owners[b] == me, 1.0, 0.0) for b in range(owners.shape[0])])
     a_all[me, col] = a_sel[pair]
     c_all[me] = c_sel[pair]
-    pl.semaphore_wait(barrier, dp - 1 + mp - 1)
+    pl.semaphore_wait(barrier, count - 1)
 
     def a_pair(k):
         dest = lax.rem(pair + k, pairs)
@@ -221,24 +219,18 @@
     slots[me, col] = stats[...]
     pre[...] = mine.reshape(halves, rows, B)
 
-    def over_mp(k):
-        return pltpu.make_async_remote_copy(
-            stats, slots.at[me, col], m_send.at[k], m_recv.at[col], (me, lax.rem(col + k, mp)), MESH)
-
-    def over_dp(k):
-        return pltpu.make_async_remote_copy(
-            slots.at[me], slots.at[me], d_send.at[k], d_recv.at[me], (lax.rem(me + k, dp), col), MESH)
-
-    for k in range(1, mp):
-        over_mp(k).start()
-    for k in range(1, mp):
-        who = lax.rem(col + k, mp)
-        pltpu.make_async_copy(stats, stats, m_recv.at[who]).wait()
-    for k in range(1, dp):
-        over_dp(k).start()
-    for k in range(1, dp):
-        who = lax.rem(me + k, dp)
-        pltpu.make_async_copy(slots.at[who], slots.at[who], d_recv.at[who]).wait()
+    def share(k):
+        return pltpu.make_async_remote_copy(
+            stats, slots.at[me, col], d_send.at[k], d_recv.at[flat], peer(k), MESH)
+
+    @pl.loop(1, count)
+    def _(k):
+        share(k).start()
+
+    @pl.loop(1, count)
+    def _(k):
+        pltpu.make_async_copy(stats, stats, d_recv.at[lax.rem(flat + k, count)]).wait()
+
     totals = jnp.sum(slots[...].reshape(dp * mp, *stats.shape), axis=0)
     grad_total = totals[0:1, 0:1]
     pre_total = totals[1:2, 0:1]
@@ -259,7 +251,7 @@
         pltpu.make_async_copy(got.at[who], got.at[who], u_recv.at[who]).wait()
     for c in range(CB):
         holder = owners[(pair // halves) * CB + c] // 2
-        update[c] = got[holder]
+        update[:, c * B : (c + 1) * B] = got[holder]
     @pl.loop(0, dp)
     def _(src):
         @pl.loop(1, mp)
@@ -274,10 +266,11 @@
         a_pair(k).wait_send()
         for h in range(CHUNKS):
             c_pair(k, h).wait_send()
-    for k in range(1, mp):
-        over_mp(k).wait_send()
-    for k in range(1, dp):
-        over_dp(k).wait_send()
+
+    @pl.loop(1, count)
+    def _(k):
+        share(k).wait_send()
+
     for k in range(1, pairs):
         piece(k).wait_send()
 
@@ -292,22 +285,18 @@
     halves = B // rows // 2
     vmem = pl.BlockSpec(memory_space=pltpu.VMEM)
     smem = pl.BlockSpec(memory_space=pltpu.SMEM)
-    anywhere = pl.BlockSpec(memory_space=pl.ANY)
     dma = pltpu.SemaphoreType.DMA
     update, root, scale, graft = pl.pallas_call(
         functools.partial(step_kernel, dp, mp),
         out_shape=(
-            jax.ShapeDtypeStruct((CB, rows, B), jnp.bfloat16),
+            jax.ShapeDtypeStruct((rows, CB * B), jnp.bfloat16),
             jax.ShapeDtypeStruct((B, B), jnp.float32),
             jax.ShapeDtypeStruct((1, 1), jnp.float32),
             jax.ShapeDtypeStruct((1, 1), jnp.float32),
         ),
-        in_specs=[smem, anywhere, anywhere],
+        in_specs=[smem, vmem, vmem],
         out_specs=(vmem, vmem, smem, smem),
         scratch_shapes=[
-            pltpu.VMEM(activations.shape, jnp.bfloat16),
-            pltpu.VMEM(cotangents.shape, jnp.bfloat16),
-            dma((2,)),
             pltpu.VMEM((B, B), jnp.float32),
             pltpu.VMEM((B, B), jnp.float32),
             pltpu.VMEM((pairs, part, B), jnp.bfloat16),
@@ -320,11 +309,11 @@
             pltpu.VMEM((halves, rows, B), jnp.bfloat16),
             pltpu.VMEM((pairs, rows, B), jnp.bfloat16),
             dma((pairs,)), dma((pairs,)), dma((dp, mp)), dma((pairs, CHUNKS)), dma((pairs, CHUNKS)), dma((dp, mp)), dma((dp, CHUNKS)),
-            dma((mp,)), dma((mp,)), dma((dp,)), dma((dp,)), dma((pairs,)), dma((pairs,)),
+            dma((dp * mp,)), dma((dp * mp,)), dma((pairs,)), dma((pairs,)),
         ],
-        compiler_params=pltpu.CompilerParams(collective_id=0, has_side_effects=True),
+        compiler_params=pltpu.CompilerParams(collective_id=0, has_side_effects=True, vmem_limit_bytes=48 * 1024 * 1024),
     )(owners, activations, cotangents)
-    return (jnp.concatenate([update[c] for c in range(CB)], axis=1), root * scale, graft[0, 0])
+    return (update, root * scale, graft[0, 0])
 
 
 def solution(mesh):

time: 66.1 us -> 65.7 us (level)
  local copies, waits for them, and re-layouts: 1.08 us -> 3.25 us
  Pallas kernels: 60.1 us -> 58.1 us
  other arithmetic: 2.36 us -> 1.67 us
    unnamed x2 -> x7, local copies, waits for them, and re-layouts: 0.01 us -> 3.25 us
    pallas_call x1, Pallas kernels: 60.1 us -> 58.1 us  [on_device(): pl.pallas_call(functools.partial(step_kernel, dp, mp), out_shape=(jax.Sha...]
    squeeze x1 -> x0, local copies, waits for them, and re-layouts: 1.07 us -> none  [on_device(): update[c]]
    concatenate x1 -> x0, other arithmetic: 0.73 us -> none  [on_device(): jnp.concatenate([update[c] for c in range(CB)], axis=1)]
where the time goes in v5:
time: 65.7 us; the launch traced here: 65.5 us
  Pallas kernels  58.1 us (88%)
  local copies, waits for them, and re-layouts  3.25 us (5%)
  between operations  2.4 us (4%)
  other arithmetic  1.67 us (3%)
    pallas_call x1, Pallas kernels, on_device(): pl.pallas_call(functools.partial(step_kernel, dp, mp), out_shape=(jax.Sha...  58.1 us
    unnamed x7, local copies, waits for them, and re-layouts  3.25 us
    mul x1, other arithmetic, on_device(): return (update, root * scale, graft[0, 0])  1.67 us

profile of v5, /device:TPU:0, one launch (start us, length us, event | category | flops | bytes accessed | tf_op | source)
XLA Modules:
  0.0 65.5 jit_solution(9952687352231261731)
XLA Ops:
  0.6 0.0 copy-start
  0.6 0.9 %copy-done = bf16[128,1024]{1,0:T(8,128)(2,1)S(1)} copy-done((bf16[128,1024]{1,0:T(8,128)(2,1)S(1)}, bf16[128,1024]{1,0:T(8,128)(2,1)}, u32[]{:S(2)}) %copy-start) | copy-done | bytes 262168
  1.6 0.0 copy-start.1
  1.6 0.9 %copy-done.1 = bf16[128,1024]{1,0:T(8,128)(2,1)S(1)} copy-done((bf16[128,1024]{1,0:T(8,128)(2,1)S(1)}, bf16[128,1024]{1,0:T(8,128)(2,1)}, u32[]{:S(2)}) %copy-start.1) | copy-done | bytes 262168
  2.5 0.0 copy-start.2
  2.5 0.7 copy-done.2
  3.2 58.1 %shard_map.58 = (bf16[128,1024]{1,0:T(8,128)(2,1)S(1)}, f32[512,512]{1,0:T(8,128)S(1)}, f32[1,1]{1,0:T(1,128)}, f32[1,1]{1,0:T(1,128)}) custom-call(s32[4]{0:T(128)S(1)} %copy-done.2, bf16[128,1024]{1,0:T(8,128)(2,1)S(1)} %copy-done, bf16[128,1024]{1,0:T(8,128)(2,1)S(1)} %copy-done.1), custom_call_target="tpu_custom_call" | custom-call | tf_op jit(solution)/shard_map/pallas_call | solution.py:289
  61.3 1.7 %broadcast_multiply_fusion = f32[512,512]{1,0:T(8,128)} fusion(f32[512,512]{1,0:T(8,128)S(1)} %get-tuple-element.8, f32[]{:T(128)} %bitcast), kind=kLoop, calls=%fused_computation | loop fusion | flops 262144 | bytes 2097156 | tf_op jit(solution)/shard_map/mul | solution.py:316
  63.0 0.7 %copy.8 = bf16[128,1024]{1,0:T(8,128)(2,1)} copy(bf16[128,1024]{1,0:T(8,128)(2,1)S(1)} %get-tuple-element.14) | data formatting | bytes 524288
Async XLA Ops:
  0.6 1.0 %copy-start = (bf16[128,1024]{1,0:T(8,128)(2,1)S(1)}, bf16[128,1024]{1,0:T(8,128)(2,1)}, u32[]{:S(2)}) copy-start(bf16[128,1024]{1,0:T(8,128)(2,1)} %acts.1) | copy-start | bytes 786436
  1.6 0.9 %copy-start.1 = (bf16[128,1024]{1,0:T(8,128)(2,1)S(1)}, bf16[128,1024]{1,0:T(8,128)(2,1)}, u32[]{:S(2)}) copy-start(bf16[128,1024]{1,0:T(8,128)(2,1)} %cots.1) | copy-start | bytes 786436
  2.5 0.7 %copy-start.2 = (s32[4]{0:T(128)S(1)}, s32[4]{0:T(128)}, u32[]{:S(2)}) copy-start(s32[4]{0:T(128)} %owners.1) | copy-start | bytes 52

commit v6 on v5

--- a/solution.py
+++ b/solution.py
@@ -48,7 +48,7 @@
 
 
 def step_kernel(
-    dp, mp, owners, acts, cots, update, root, scale_ref, graft_ref, grad, oriented, a_sel, c_sel, a_all, c_all,
+    dp, mp, owners, acts_in, cots_in, update, root, graft_ref, acts, cots, in_sem, grad, oriented, a_sel, c_sel, a_all, c_all,
     stats, slots, pre, out, got,
     az_send, ax_send, am_send, cz_send, cx_send, a_recv, c_recv, d_send, d_recv, u_send, u_recv,
 ):
@@ -74,6 +74,15 @@
     def _(k):
         pl.semaphore_signal(barrier, inc=1, device_id=peer(k), device_id_type=MESH)
 
+
+    fetches = [
+        pltpu.make_async_copy(acts_in, acts, in_sem.at[0]),
+        pltpu.make_async_copy(cots_in, cots, in_sem.at[1]),
+    ]
+    for fetch in fetches:
+        fetch.start()
+    for fetch in fetches:
+        fetch.wait()
 
     def block_of(which):
         held = [jnp.where(owners[b] // 2 == which, b, 0) for b in range(owners.shape[0])]
@@ -206,7 +215,6 @@
     eye = jnp.where(ids[0] == ids[1], 1.0, 0.0)
     ridge = 0.1 * (grad_total / B + 1.0)
     root[...], factor = inverse_root(product(g, g, transposed=True) + ridge * eye, eye)
-    scale_ref[0, 0] = factor[0, 0]
     is_right = 1.0 - is_left
     halves, rows = out.shape[:2]
     starts = [pl.multiple_of((2 * h + side) * rows, rows) for h in range(halves)]
@@ -246,6 +254,7 @@
     for k in range(1, pairs):
         piece(k).start()
     got[pair] = out[pair % halves]
+    root[...] = root[...] * factor
     for k in range(1, pairs):
         who = lax.rem(pair + k, pairs)
         pltpu.make_async_copy(got.at[who], got.at[who], u_recv.at[who]).wait()
@@ -285,18 +294,21 @@
     halves = B // rows // 2
     vmem = pl.BlockSpec(memory_space=pltpu.VMEM)
     smem = pl.BlockSpec(memory_space=pltpu.SMEM)
+    hbm = pl.BlockSpec(memory_space=pltpu.HBM)
     dma = pltpu.SemaphoreType.DMA
-    update, root, scale, graft = pl.pallas_call(
+    update, root, graft = pl.pallas_call(
         functools.partial(step_kernel, dp, mp),
         out_shape=(
             jax.ShapeDtypeStruct((rows, CB * B), jnp.bfloat16),
             jax.ShapeDtypeStruct((B, B), jnp.float32),
             jax.ShapeDtypeStruct((1, 1), jnp.float32),
-            jax.ShapeDtypeStruct((1, 1), jnp.float32),
         ),
-        in_specs=[smem, vmem, vmem],
-        out_specs=(vmem, vmem, smem, smem),
+        in_specs=[smem, hbm, hbm],
+        out_specs=(vmem, vmem, smem),
         scratch_shapes=[
+            pltpu.VMEM(activations.shape, jnp.bfloat16),
+            pltpu.VMEM(cotangents.shape, jnp.bfloat16),
+            dma((2,)),
             pltpu.VMEM((B, B), jnp.float32),
             pltpu.VMEM((B, B), jnp.float32),
             pltpu.VMEM((pairs, part, B), jnp.bfloat16),
@@ -313,7 +325,7 @@
         ],
         compiler_params=pltpu.CompilerParams(collective_id=0, has_side_effects=True, vmem_limit_bytes=48 * 1024 * 1024),
     )(owners, activations, cotangents)
-    return (update, root * scale, graft[0, 0])
+    return (update, root, graft[0, 0])
 
 
 def solution(mesh):

time: 65.7 us -> 65 us (0.989)
  other arithmetic: 1.67 us -> 0 us
  local copies, waits for them, and re-layouts: 3.25 us -> 4.22 us
    mul x1 -> x0, other arithmetic: 1.67 us -> none  [on_device(): return (update, root * scale, graft[0, 0])]
    unnamed x7 -> x8, local copies, waits for them, and re-layouts: 3.25 us -> 4.22 us
where the time goes in v6:
time: 65 us; the launch traced here: 64.8 us
  Pallas kernels  58.2 us (90%)
  local copies, waits for them, and re-layouts  4.22 us (6%)
  between operations  2.39 us (4%)
    pallas_call x1, Pallas kernels, on_device(): pl.pallas_call(functools.partial(step_kernel, dp, mp), out_shape=(jax.Sha...  58.2 us
    unnamed x8, local copies, waits for them, and re-layouts  4.22 us

profile of v6, /device:TPU:0, one launch (start us, length us, event | category | flops | bytes accessed | tf_op | source)
XLA Modules:
  0.0 64.8 jit_solution(14053215639401900105)
XLA Ops:
  0.6 0.0 copy-start
  0.6 0.9 %copy-done = bf16[128,1024]{1,0:T(8,128)(2,1)S(1)} copy-done((bf16[128,1024]{1,0:T(8,128)(2,1)S(1)}, bf16[128,1024]{1,0:T(8,128)(2,1)}, u32[]{:S(2)}) %copy-start) | copy-done | bytes 262168
  1.6 0.0 copy-start.1
  1.6 0.9 %copy-done.1 = bf16[128,1024]{1,0:T(8,128)(2,1)S(1)} copy-done((bf16[128,1024]{1,0:T(8,128)(2,1)S(1)}, bf16[128,1024]{1,0:T(8,128)(2,1)}, u32[]{:S(2)}) %copy-start.1) | copy-done | bytes 262168
  2.5 0.0 copy-start.2
  2.5 0.7 %copy-done.2 = s32[4]{0:T(128)S(1)} copy-done((s32[4]{0:T(128)S(1)}, s32[4]{0:T(128)}, u32[]{:S(2)}) %copy-start.2) | copy-done | bytes 40
  3.2 58.2 %shard_map.58 = (bf16[128,1024]{1,0:T(8,128)(2,1)S(1)}, f32[512,512]{1,0:T(8,128)S(1)}, f32[1,1]{1,0:T(1,128)}) custom-call(s32[4]{0:T(128)S(1)} %copy-done.2, bf16[128,1024]{1,0:T(8,128)(2,1)S(1)} %copy-done, bf16[128,1024]{1,0:T(8,128)(2,1)S(1)} %copy-done.1), custom_call_target="tpu_custom_call" | custom-call | tf_op jit(solution)/shard_map/pallas_call | solution.py:299
  61.4 0.7 %copy.9 = bf16[128,1024]{1,0:T(8,128)(2,1)} copy(bf16[128,1024]{1,0:T(8,128)(2,1)S(1)} %get-tuple-element.12) | data formatting | bytes 524288
  62.1 1.0 %copy.10 = f32[512,512]{1,0:T(8,128)} copy(f32[512,512]{1,0:T(8,128)S(1)} %get-tuple-element.13) | data formatting | bytes 2097152
Async XLA Ops:
  0.6 1.0 %copy-start = (bf16[128,1024]{1,0:T(8,128)(2,1)S(1)}, bf16[128,1024]{1,0:T(8,128)(2,1)}, u32[]{:S(2)}) copy-start(bf16[128,1024]{1,0:T(8,128)(2,1)} %acts_in.1) | copy-start | bytes 786436
  1.6 0.9 %copy-start.1 = (bf16[128,1024]{1,0:T(8,128)(2,1)S(1)}, bf16[128,1024]{1,0:T(8,128)(2,1)}, u32[]{:S(2)}) copy-start(bf16[128,1024]{1,0:T(8,128)(2,1)} %cots_in.1) | copy-start | bytes 786436
  2.5 0.7 %copy-start.2 = (s32[4]{0:T(128)S(1)}, s32[4]{0:T(128)}, u32[]{:S(2)}) copy-start(s32[4]{0:T(128)} %owners.1) | copy-start | bytes 52
